TPU v7x, 512 devices: a 4x2x32 block of a 4x16x32 slice. The times are simulated.
512 devices in a mesh: ens: 2 (over y), gx: 64 (over z, core), gy: 4 (over x).
Axes of the slice: x: 4, y: 2, z: 32, core: 2. Of those that a mesh axis runs over, the one named last changes fastest.
The devices are a block of a 4x16x32 slice.
Arguments:
- log_cond: float32 [1024, 512, 128], P(('ens', 'gx'), 'gy'), parts along dimension 0, may hold values from -1 to 1
- checkpoint: float32 [1024, 512, 128], P(('ens', 'gx'), 'gy'), parts along dimension 0, may hold values from 0 to 1
- survey: float32 [1024, 512, 128], P(('ens', 'gx'), 'gy'), parts along dimension 0, may hold values from 0 to 1
- survey_weight: float32 [1024, 512, 128], P(('ens', 'gx'), 'gy'), parts along dimension 0, may hold values from 0.5 to 5
- well_cells: int32 [512], P('ens'), parts along dimension 0, may hold values from 0 to 33554431
- well_data: float32 [512], P('ens'), parts along dimension 0, may hold values from 0 to 1
- well_weight: float32 [512], P('ens'), parts along dimension 0, may hold values from 1 to 10
- source_cells: int32 [128], P('ens'), parts along dimension 0, may hold values from 0 to 33554431
- source_rate: float32 [128], P('ens'), parts along dimension 0, may hold values from 5 to 20
- step_number: int32 [2], P('ens'), parts along dimension 0, may hold values from 0 to 1999
Outputs:
- log_cond_grad: float32 [1024, 512, 128], P(('ens', 'gx'), 'gy'), parts along dimension 0
- checkpoint_adjoint: float32 [1024, 512, 128], P(('ens', 'gx'), 'gy'), parts along dimension 0
- concentration: float32 [1024, 512, 128], P(('ens', 'gx'), 'gy'), parts along dimension 0
- misfit: float32 [2], P('ens'), parts along dimension 0
There are 2 independent parts, one for each index of `ens`. A program takes and returns all parts, laid end to end along the dimension named above; each array names one. Nothing has to cross between parts.
Inputs may be any that keep to these rules, and one draw needn't show every extreme that they name: `well_cells`: flat cell index (x * 512 + y) * 128 + z. `source_cells`: flat cell index (x * 512 + y) * 128 + z.
All inputs are finite; a program needn't handle non-finite values.
Results may differ from a plain program's by a relative error of at most 0.00002.
Values sent between devices are 32-bit elements; how exact they have to be, the bound alone decides.
No kernel may reach another device: no remote copies, remote signals or barrier semaphores. Data moves between devices by JAX's collectives and lax.ppermute only.
A program may use at most 64 MiB of HBM per device.

v0:
```python
import jax
import jax.numpy as jnp
from jax import lax
from jax.sharding import Mesh
from jax.sharding import PartitionSpec as P

GX = ("gx_0", "gx_1")
ENS_GX = ("ens", "gx_0", "gx_1")


time_step = 0.2
head_slope = 0.5
molecular = 0.05
dispersivity = 0.1


def extended(block, sides, width):
    for axis, dim in sides:
        count = lax.axis_size(axis)
        forward = [(i, i + 1) for i in range(count - 1)]
        backward = [(target, source) for source, target in forward]
        low = lax.ppermute(
            lax.slice_in_dim(block, block.shape[dim] - width, None, axis=dim), axis, forward
        )
        high = lax.ppermute(lax.slice_in_dim(block, 0, width, axis=dim), axis, backward)
        block = jnp.concatenate([low, block, high], axis=dim)
    return block


def from_everyone(shard, axis):
    count = lax.axis_size(axis)
    return lax.all_to_all(
        jnp.broadcast_to(shard[None], (count, *shard.shape)), axis, 0, 0, tiled=True
    )


def taken_together(shard, axis):
    everything = from_everyone(shard, axis)
    return jnp.sum(everything, axis=0)


def one_axis_at_a_time(shard, axes):
    far, near = axes
    return taken_together(taken_together(shard, near), far)


def validity(extent, rim_width, position, grid_total):
    global_pos = position * extent - rim_width + jnp.arange(extent + 2 * rim_width, dtype=jnp.int32)
    return ((global_pos >= 0) & (global_pos < grid_total)).astype(jnp.float32)


def face_terms(log_cond, mask_x, mask_y):
    cond_x = jnp.exp(0.5 * (log_cond[:-1] + log_cond[1:]))
    cond_y = jnp.exp(0.5 * (log_cond[:, :-1] + log_cond[:, 1:]))
    cond_z = jnp.exp(0.5 * (log_cond[:, :, :-1] + log_cond[:, :, 1:]))
    open_x = (mask_x[:-1] * mask_x[1:])[:, None, None]
    open_y = (mask_y[:-1] * mask_y[1:])[None, :, None]
    return (cond_x, cond_y, cond_z, open_x, open_y)


def forward_step(tracer, log_cond, mask_x, mask_y, source):
    cond_x, cond_y, cond_z, open_x, open_y = face_terms(log_cond, mask_x, mask_y)
    flux_x = open_x * (
        head_slope * cond_x * tracer[:-1]
        - (molecular + dispersivity * cond_x) * (tracer[1:] - tracer[:-1])
    )
    flux_y = open_y * (-(molecular + dispersivity * cond_y) * (tracer[:, 1:] - tracer[:, :-1]))
    flux_z = -(molecular + dispersivity * cond_z) * (tracer[:, :, 1:] - tracer[:, :, :-1])
    div_x = (flux_x[1:] - flux_x[:-1])[:, 1:-1]
    div_y = (flux_y[:, 1:] - flux_y[:, :-1])[1:-1]
    padded_z = jnp.pad(flux_z, ((0, 0), (0, 0), (1, 1)))
    div_z = (padded_z[:, :, 1:] - padded_z[:, :, :-1])[1:-1, 1:-1]
    return tracer[1:-1, 1:-1] - time_step * (div_x + div_y + div_z) + time_step * source[1:-1, 1:-1]


def adjoint_step(adjoint, tracer, log_cond, mask_x, mask_y):
    cond_x, cond_y, cond_z, open_x, open_y = face_terms(log_cond, mask_x, mask_y)
    disp_x = molecular + dispersivity * cond_x
    disp_y = molecular + dispersivity * cond_y
    disp_z = molecular + dispersivity * cond_z
    jump_x = open_x * time_step * (adjoint[1:] - adjoint[:-1])
    jump_y = open_y * time_step * (adjoint[:, 1:] - adjoint[:, :-1])
    jump_z = time_step * (adjoint[:, :, 1:] - adjoint[:, :, :-1])
    push_x = jump_x * (head_slope * cond_x + disp_x)
    pull_x = -jump_x * disp_x
    push_y = jump_y * disp_y
    pull_y = -jump_y * disp_y
    push_z = jnp.pad(jump_z * disp_z, ((0, 0), (0, 0), (1, 1)))
    pull_z = jnp.pad(-jump_z * disp_z, ((0, 0), (0, 0), (1, 1)))
    sens_x = (
        jump_x
        * (head_slope * tracer[:-1] - dispersivity * (tracer[1:] - tracer[:-1]))
        * 0.5
        * cond_x
    )
    sens_y = jump_y * (-dispersivity * (tracer[:, 1:] - tracer[:, :-1])) * 0.5 * cond_y
    sens_z = jnp.pad(
        jump_z * (-dispersivity * (tracer[:, :, 1:] - tracer[:, :, :-1])) * 0.5 * cond_z,
        ((0, 0), (0, 0), (1, 1)),
    )
    updated = (
        adjoint[1:-1, 1:-1]
        + (push_x[1:] + pull_x[:-1])[:, 1:-1]
        + (push_y[:, 1:] + pull_y[:, :-1])[1:-1]
    )
    updated = updated + (push_z[:, :, 1:] + pull_z[:, :, :-1])[1:-1, 1:-1]
    gradient = (sens_x[1:] + sens_x[:-1])[:, 1:-1] + (sens_y[:, 1:] + sens_y[:, :-1])[1:-1]
    gradient = gradient + (sens_z[:, :, 1:] + sens_z[:, :, :-1])[1:-1, 1:-1]
    return (updated, gradient)


def locate(cells, start_x, start_y, extent_x, extent_y, grid_y, grid_z):
    along_x = cells // (grid_y * grid_z) - start_x
    along_y = cells // grid_z % grid_y - start_y
    along_z = cells % grid_z
    inside = ((along_x >= 0) & (along_x < extent_x) & (along_y >= 0) & (along_y < extent_y)).astype(
        jnp.float32
    )
    return (jnp.clip(along_x, 0, extent_x - 1), jnp.clip(along_y, 0, extent_y - 1), along_z, inside)


def on_device(
    log_cond,
    checkpoint,
    survey,
    survey_weight,
    well_cells,
    well_data,
    well_weight,
    source_cells,
    source_rate,
    step_number,
):
    local_x, local_y, extent_z = checkpoint.shape
    grid_x = local_x * lax.axis_size(GX)
    grid_y = local_y * lax.axis_size("gy")
    place_x = lax.axis_index(GX)
    place_y = lax.axis_index("gy")
    anchor_x = place_x * local_x
    anchor_y = place_y * local_y
    clock = step_number.astype(jnp.float32)[0]
    rate_first = source_rate * (1.0 + 0.5 * jnp.sin(0.05 * clock))
    rate_second = source_rate * (1.0 + 0.5 * jnp.sin(0.05 * (clock + 1.0)))

    def masks(rim_width):
        return (
            validity(local_x, rim_width, place_x, grid_x),
            validity(local_y, rim_width, place_y, grid_y),
        )

    def sources(rates, rim_width):
        extent_x = local_x + 2 * rim_width
        extent_y = local_y + 2 * rim_width
        spot_x, spot_y, spot_z, inside = locate(
            source_cells,
            anchor_x - rim_width,
            anchor_y - rim_width,
            extent_x,
            extent_y,
            grid_y,
            extent_z,
        )
        blank = jnp.zeros((extent_x, extent_y, extent_z), jnp.float32)
        return blank.at[spot_x, spot_y, spot_z].add(rates * inside)

    stacked = jnp.stack((checkpoint, log_cond))
    padded = extended(stacked, ((GX, 1), ("gy", 2)), 3)
    state_zero = padded[0]
    cond_pad = padded[1]
    mask_x3, mask_y3 = masks(3)
    state_one = forward_step(state_zero, cond_pad, mask_x3, mask_y3, sources(rate_first, 3))
    mask_x2, mask_y2 = masks(2)
    cond_two = cond_pad[1:-1, 1:-1]
    final_wide = forward_step(state_one, cond_two, mask_x2, mask_y2, sources(rate_second, 2))
    final = final_wide[1:-1, 1:-1]
    missed = final - survey
    seed = survey_weight * missed
    spot_x, spot_y, spot_z, owned = locate(
        well_cells, anchor_x, anchor_y, local_x, local_y, grid_y, extent_z
    )
    nearby = final[spot_x, spot_y, spot_z] - well_data
    seed = seed.at[spot_x, spot_y, spot_z].add(well_weight * nearby * owned)
    partial_value = jnp.sum(survey_weight * missed * missed) + jnp.sum(
        owned * well_weight * nearby * nearby
    )
    seed, partial_value = (seed, partial_value)
    seed_pad = extended(seed, ((GX, 0), ("gy", 1)), 2)
    adjoint_one, sens_wide = adjoint_step(seed_pad, state_one, cond_two, mask_x2, mask_y2)
    sens_one = sens_wide[1:-1, 1:-1]
    mask_x1, mask_y1 = masks(1)
    adjoint_zero, sens_zero = adjoint_step(
        adjoint_one, state_zero[2:-2, 2:-2], cond_pad[2:-2, 2:-2], mask_x1, mask_y1
    )
    total = one_axis_at_a_time(partial_value, ("gx_0", ("gx_1", "gy")))
    misfit = (0.5 * total / (grid_x * grid_y * extent_z)).reshape(1)
    return (sens_one + sens_zero, adjoint_zero, final, misfit)


def solution(mesh):
    finer = Mesh(
        mesh.devices.reshape(mesh.shape["ens"], 32, 2, mesh.shape["gy"]),
        ("ens", "gx_0", "gx_1", "gy"),
    )
    return jax.shard_map(
        on_device,
        mesh=finer,
        in_specs=(
            P(ENS_GX, "gy", None),
            P(ENS_GX, "gy", None),
            P(ENS_GX, "gy", None),
            P(ENS_GX, "gy", None),
            P("ens"),
            P("ens"),
            P("ens"),
            P("ens"),
            P("ens"),
            P("ens"),
        ),
        out_specs=(P(ENS_GX, "gy", None), P(ENS_GX, "gy", None), P(ENS_GX, "gy", None), P("ens")),
        check_vma=False,
    )
```

profile of v0, /device:TPU:40, one launch (start us, length us, event | category | flops | bytes accessed | tf_op | source)
XLA Modules:
  0.0 174.3 jit_solution(14538910791826176606)
XLA Ops:
  0.7 1.3 pad_maximum_fusion.3
  2.0 1.3 collective-permute-start.1
  3.3 3.1 %collective-permute-start = (f32[2,3,128,128]{3,2,1,0:T(8,128)S(1)}, f32[2,3,128,128]{3,2,1,0:T(8,128)S(1)}, u32[]{:S(2)}, u32[]{:S(2)}) collective-permute-start(f32[2,3,128,128]{3,2,1,0:T(8,128)S(1)} %get-tuple-element.47), channel_id=1, source_target_pairs={{0,4},{4,8},{8,12},{12,16},{16,20},{20,24},{24,28},{28,32},{32,36}... | collective-permute-start | bytes 1179656 | tf_op jit(solution)/shard_map/ppermute | solution.py:22
  7.4 0.7 and_select_fusion.5
  8.1 0.7 fusion.93
  9.6 0.7 compare_select_fusion.2
  10.5 1.3 collective-permute-start.3
  11.8 4.6 %collective-permute-start.2 = (f32[2,14,3,128]{3,2,1,0:T(4,128)S(1)}, f32[2,14,3,128]{3,2,1,0:T(4,128)S(1)}, u32[]{:S(2)}, u32[]{:S(2)}) collective-permute-start(f32[2,14,3,128]{3,2,1,0:T(4,128)S(1)} %get-tuple-element.39), channel_id=1, source_target_pairs={{0,1},{1,2},{2,3},{4,5},{5,6},{6,7},{8,9},{9,10},{10,11},{12,13},{... | collective-permute-start | bytes 129032 | tf_op jit(solution)/shard_map/ppermute | solution.py:22
  16.6 4.5 %scatter_fusion.1 = f32[12,132,128]{2,1,0:T(8,128)S(1)} fusion(f32[12,132,128]{2,1,0:T(8,128)S(1)} %broadcast_in_dim.28, s32[64]{0:T(128)S(1)} %get-tuple-element.97, f32[64]{0:T(128)S(1)} %and_select_fusion.4), kind=kCustom, calls=%fused_computation.2 | custom fusion | flops 64 | bytes 1536 | tf_op jit(solution)/shard_map/scatter-add | solution.py:164
  21.2 4.5 %scatter_fusion = f32[14,134,128]{2,1,0:T(8,128)S(1)} fusion(f32[14,134,128]{2,1,0:T(8,128)S(1)} %broadcast_in_dim.24, s32[64]{0:T(128)S(1)} %get-tuple-element.98, f32[64]{0:T(128)S(1)} %get-tuple-element.34), kind=kCustom, calls=%fused_computation.1 | custom fusion | flops 64 | bytes 1536 | tf_op jit(solution)/shard_map/scatter-add | solution.py:164
  25.8 0.9 copy-done.2
  26.8 1.2 pad_maximum_fusion
  28.1 1.1 broadcast_multiply_fusion
  31.2 1.1 copy-done.3
  32.3 0.7 fusion.25
  33.0 1.4 negate_multiply_fusion.1
  34.9 1.4 multiply_multiply_fusion.2
  36.7 0.8 copy-done.18
  37.6 1.3 fusion.103
  38.9 0.7 multiply_reduce_fusion
  39.7 8.9 %gather_fusion = f32[256]{0:T(256)S(1)} fusion(f32[8,128,128]{2,1,0:T(8,128)} %get-tuple-element.29, s32[256]{0:T(256)S(1)} %bitcast.53), kind=kCustom, calls=%fused_computation | custom fusion | bytes 5120 | tf_op jit(solution)/shard_map/gather | solution.py:181
  49.2 15.4 %scatter_fusion.2 = f32[8,128,128]{2,1,0:T(8,128)S(1)} fusion(f32[8,128,128]{2,1,0:T(8,128)S(1)} %get-tuple-element.5, s32[256]{0:T(256)S(1)} %bitcast.52, f32[256]{0:T(256)S(1)} %get-tuple-element.96), kind=kCustom, calls=%fused_computation.3 | custom fusion | flops 256 | bytes 6144 | tf_op jit(solution)/shard_map/scatter-add | solution.py:182
  64.6 0.7 fusion.123
  65.4 4.2 %collective-permute-start.4 = (f32[2,128,128]{2,1,0:T(8,128)}, f32[2,128,128]{2,1,0:T(8,128)S(1)}, u32[]{:S(2)}, u32[]{:S(2)}) collective-permute-start(f32[2,128,128]{2,1,0:T(8,128)} %get-tuple-element.94), channel_id=1, source_target_pairs={{0,4},{4,8},{8,12},{12,16},{16,20},{20,24},{24,28},{28,32},{32,36}... | collective-permute-start | bytes 393224 | tf_op jit(solution)/shard_map/ppermute | solution.py:22
  69.5 2.7 %fusion.110 = (f32[12,130,128]{2,1,0:T(8,128)}, f32[12,130,128]{2,1,0:T(8,128)}) fusion(f32[12,131,128]{2,1,0:T(8,128)} %get-tuple-element.31), kind=kLoop, calls=%fused_computation.265 | loop fusion | bytes 3194880 | tf_op jit(solution)/shard_map/slice | solution.py:104
  72.2 1.2 multiply_add_fusion.5
  73.4 1.3 collective-permute-start.5
  76.0 12.4 %all_to_all.12 = f32[8,1,1]{2,1,0:T(1,128)S(1)} all-to-all(f32[8,1,1]{2,1,0:T(1,128)S(1)} %broadcast_in_dim.64), channel_id=1, replica_groups=mesh['ens'=2,'gx_0'=32,'gx_1'=2,'gy'=4] {'gx_1','gy'}, dimensions={0} | all-to-all | bytes 64 | tf_op jit(solution)/shard_map/all_to_all | solution.py:32
  89.0 1.3 broadcast_in_dim.65
  90.3 45.6 %all-to-all-start.1 = ((f32[32,1,1]{2,1,0:T(1,128)}), f32[32,1,1]{2,1,0:T(1,128)S(1)}, u32[]{:S(2)}, u32[]{:S(2)}) async-start(f32[32,1,1]{2,1,0:T(1,128)} %broadcast_in_dim.65), calls=%async_computation.1 | async-start | bytes 32768 | tf_op jit(solution)/shard_map/all_to_all | solution.py:32
  135.9 0.7 constant_dynamic-update-slice_fusion.2
  136.6 0.8 constant_dynamic-update-slice_fusion.1
  137.4 1.6 constant_dynamic-update-slice_fusion
  139.0 0.8 fusion.112
  139.9 1.3 collective-permute-start.7
  141.2 4.6 %collective-permute-start.6 = (f32[12,2,128]{2,1,0:T(2,128)S(1)}, f32[12,2,128]{2,1,0:T(2,128)S(1)}, u32[]{:S(2)}, u32[]{:S(2)}) collective-permute-start(f32[12,2,128]{2,1,0:T(2,128)S(1)} %get-tuple-element.68), channel_id=1, source_target_pairs={{0,1},{1,2},{2,3},{4,5},{5,6},{6,7},{8,9},{9,10},{10,11},{12,13},{... | collective-permute-start | bytes 36872 | tf_op jit(solution)/shard_map/ppermute | solution.py:22
  145.8 1.1 fusion.120
  146.9 0.9 slice.680
  147.8 0.9 slice.729
  148.7 8.8 %all-to-all-done.1 = f32[32,1,1]{2,1,0:T(1,128)S(1)} async-done(((f32[32,1,1]{2,1,0:T(1,128)}), f32[32,1,1]{2,1,0:T(1,128)S(1)}, u32[]{:S(2)}, u32[]{:S(2)}) %all-to-all-start.1) | async-done | bytes 160 | tf_op jit(solution)/shard_map/all_to_all | solution.py:32
  158.8 1.3 pad_maximum_fusion.1
  161.8 1.0 copy-done.1
  163.4 1.0 copy-done.9
  164.8 0.9 fusion.47
  165.7 0.8 fusion.61
  169.0 0.8 copy-done.13
  170.1 1.5 fusion.62
  171.6 1.6 fusion.68
  (102 shorter events, 11.7 us)
Async XLA Ops:
  0.6 9.8 %copy-start.6 = (f32[8,128,128]{2,1,0:T(8,128)S(1)}, f32[8,128,128]{2,1,0:T(8,128)}, u32[]{:S(2)}) copy-start(f32[8,128,128]{2,1,0:T(8,128)} %param.10) | copy-start | bytes 1572868
  0.6 9.8 %copy-start.7 = (f32[8,128,128]{2,1,0:T(8,128)S(1)}, f32[8,128,128]{2,1,0:T(8,128)}, u32[]{:S(2)}) copy-start(f32[8,128,128]{2,1,0:T(8,128)} %param.11) | copy-start | bytes 1572868
  2.0 8.4 %collective-permute-start.1 = (f32[2,3,128,128]{3,2,1,0:T(8,128)S(1)}, f32[2,3,128,128]{3,2,1,0:T(8,128)S(1)}, u32[]{:S(2)}, u32[]{:S(2)}) collective-permute-start(f32[2,3,128,128]{3,2,1,0:T(8,128)S(1)} %get-tuple-element.48), channel_id=1, source_target_pairs={{4,0},{8,4},{12,8},{16,12},{20,16},{24,20},{28,24},{32,28},{36,32}... | collective-permute-start | bytes 1179656 | tf_op jit(solution)/shard_map/ppermute | solution.py:25
  3.3 7.1 %collective-permute-start = (f32[2,3,128,128]{3,2,1,0:T(8,128)S(1)}, f32[2,3,128,128]{3,2,1,0:T(8,128)S(1)}, u32[]{:S(2)}, u32[]{:S(2)}) collective-permute-start(f32[2,3,128,128]{3,2,1,0:T(8,128)S(1)} %get-tuple-element.47), channel_id=1, source_target_pairs={{0,4},{4,8},{8,12},{12,16},{16,20},{20,24},{24,28},{28,32},{32,36}... | collective-permute-start | bytes 1179656 | tf_op jit(solution)/shard_map/ppermute | solution.py:22
  10.5 6.0 %copy-start.16 = (f32[2,3,128,128]{3,2,1,0:T(8,128)}, f32[2,3,128,128]{3,2,1,0:T(8,128)S(1)}, u32[]{:S(2)}) copy-start(f32[2,3,128,128]{3,2,1,0:T(8,128)S(1)} %collective-permute-done) | copy-start | bytes 1179652
  10.5 15.3 %collective-permute-start.3 = (f32[2,14,3,128]{3,2,1,0:T(4,128)S(1)}, f32[2,14,3,128]{3,2,1,0:T(4,128)S(1)}, u32[]{:S(2)}, u32[]{:S(2)}) collective-permute-start(f32[2,14,3,128]{3,2,1,0:T(4,128)S(1)} %get-tuple-element.40), channel_id=1, source_target_pairs={{1,0},{2,1},{3,2},{5,4},{6,5},{7,6},{9,8},{10,9},{11,10},{13,12},{... | collective-permute-start | bytes 129032 | tf_op jit(solution)/shard_map/ppermute | solution.py:25
  11.8 14.0 %collective-permute-start.2 = (f32[2,14,3,128]{3,2,1,0:T(4,128)S(1)}, f32[2,14,3,128]{3,2,1,0:T(4,128)S(1)}, u32[]{:S(2)}, u32[]{:S(2)}) collective-permute-start(f32[2,14,3,128]{3,2,1,0:T(4,128)S(1)} %get-tuple-element.39), channel_id=1, source_target_pairs={{0,1},{1,2},{2,3},{4,5},{5,6},{6,7},{8,9},{9,10},{10,11},{12,13},{... | collective-permute-start | bytes 129032 | tf_op jit(solution)/shard_map/ppermute | solution.py:22
  25.8 1.0 copy-start.2
  29.2 7.1 %copy-start = (f32[11,132,128]{2,1,0:T(8,128)}, f32[11,132,128]{2,1,0:T(8,128)S(1)}, u32[]{:S(2)}) copy-start(f32[11,132,128]{2,1,0:T(8,128)S(1)} %get-tuple-element.17) | copy-start | bytes 2230276
  31.1 1.2 copy-start.3
  36.5 1.0 copy-start.18
  37.6 1.4 copy-start.17
  38.9 9.7 %copy-start.19 = (f32[256]{0:T(256)S(1)}, f32[256]{0:T(256)}, u32[]{:S(2)}) copy-start(f32[256]{0:T(256)} %param.16) | copy-start | bytes 3076
  38.9 9.7 %copy-start.20 = (f32[256]{0:T(256)S(1)}, f32[256]{0:T(256)}, u32[]{:S(2)}) copy-start(f32[256]{0:T(256)} %param.15) | copy-start | bytes 3076
  65.4 70.5 %collective-permute-start.4 = (f32[2,128,128]{2,1,0:T(8,128)}, f32[2,128,128]{2,1,0:T(8,128)S(1)}, u32[]{:S(2)}, u32[]{:S(2)}) collective-permute-start(f32[2,128,128]{2,1,0:T(8,128)} %get-tuple-element.94), channel_id=1, source_target_pairs={{0,4},{4,8},{8,12},{12,16},{16,20},{20,24},{24,28},{28,32},{32,36}... | collective-permute-start | bytes 393224 | tf_op jit(solution)/shard_map/ppermute | solution.py:22
  73.4 64.0 %collective-permute-start.5 = (f32[2,128,128]{2,1,0:T(8,128)}, f32[2,128,128]{2,1,0:T(8,128)}, u32[]{:S(2)}, u32[]{:S(2)}) collective-permute-start(f32[2,128,128]{2,1,0:T(8,128)} %get-tuple-element.93), channel_id=1, source_target_pairs={{4,0},{8,4},{12,8},{16,12},{20,16},{24,20},{28,24},{32,28},{36,32}... | collective-permute-start | bytes 393224 | tf_op jit(solution)/shard_map/ppermute | solution.py:25
  90.3 67.2 %all-to-all-start.1 = ((f32[32,1,1]{2,1,0:T(1,128)}), f32[32,1,1]{2,1,0:T(1,128)S(1)}, u32[]{:S(2)}, u32[]{:S(2)}) async-start(f32[32,1,1]{2,1,0:T(1,128)} %broadcast_in_dim.65), calls=%async_computation.1 | async-start | bytes 32768 | tf_op jit(solution)/shard_map/all_to_all | solution.py:32
  135.9 9.9 %copy-start.5 = (f32[9,130,128]{2,1,0:T(8,128)S(1)}, f32[9,130,128]{2,1,0:T(8,128)}, u32[]{:S(2)}) copy-start(f32[9,130,128]{2,1,0:T(8,128)} %get-tuple-element.6) | copy-start | bytes 1797124
  135.9 11.0 %copy-start.11 = (f32[11,132,128]{2,1,0:T(8,128)S(1)}, f32[11,132,128]{2,1,0:T(8,128)}, u32[]{:S(2)}) copy-start(f32[11,132,128]{2,1,0:T(8,128)} %get-tuple-element.16) | copy-start | bytes 2230276
  137.4 10.4 %copy-start.4 = (f32[9,130,128]{2,1,0:T(8,128)S(1)}, f32[9,130,128]{2,1,0:T(8,128)}, u32[]{:S(2)}) copy-start(f32[9,130,128]{2,1,0:T(8,128)} %get-tuple-element.7) | copy-start | bytes 1797124
  139.9 18.9 %collective-permute-start.7 = (f32[12,2,128]{2,1,0:T(2,128)S(1)}, f32[12,2,128]{2,1,0:T(2,128)S(1)}, u32[]{:S(2)}, u32[]{:S(2)}) collective-permute-start(f32[12,2,128]{2,1,0:T(2,128)S(1)} %get-tuple-element.69), channel_id=1, source_target_pairs={{1,0},{2,1},{3,2},{5,4},{6,5},{7,6},{9,8},{10,9},{11,10},{13,12},{... | collective-permute-start | bytes 36872 | tf_op jit(solution)/shard_map/ppermute | solution.py:25
  141.2 17.6 %collective-permute-start.6 = (f32[12,2,128]{2,1,0:T(2,128)S(1)}, f32[12,2,128]{2,1,0:T(2,128)S(1)}, u32[]{:S(2)}, u32[]{:S(2)}) collective-permute-start(f32[12,2,128]{2,1,0:T(2,128)S(1)} %get-tuple-element.68), channel_id=1, source_target_pairs={{0,1},{1,2},{2,3},{4,5},{5,6},{6,7},{8,9},{9,10},{10,11},{12,13},{... | collective-permute-start | bytes 36872 | tf_op jit(solution)/shard_map/ppermute | solution.py:22
  158.8 1.4 copy-start.8
  161.7 1.1 copy-start.1
  163.2 1.2 copy-start.9
  163.2 1.4 copy-start.10
  163.2 1.6 copy-start.12
  168.7 1.1 copy-start.13
  168.7 1.2 copy-start.14
  168.8 1.4 copy-start.15
where the time goes:
time: 175 us; the launch traced here: 174 us
  starting transfers between devices  67.3 us (38%)
  other arithmetic  49.9 us (29%)
  local copies, waits for them, and re-layouts  30.7 us (18%)
  blocking collectives  12.4 us (7%)
  waiting for transfers between devices  8.84 us (5%)
  between operations  5.15 us (3%)
    all_to_all x1, starting transfers between devices, from_everyone(): lax.all_to_all(jnp.broadcast_to(shard[None], (count, *shard.shape)), axis...  45.6 us
    ppermute x4, starting transfers between devices, extended(): lax.ppermute(lax.slice_in_dim(block, block.shape[dim] - width, None, axis...  16.5 us
    scatter-add x1, other arithmetic, on_device(): seed = seed.at[spot_x, spot_y, spot_z].add(well_weight * nearby * owned)  15.4 us
    all_to_all x1, blocking collectives, from_everyone(): lax.all_to_all(jnp.broadcast_to(shard[None], (count, *shard.shape)), axis...  12.4 us
    scatter-add x2, other arithmetic, sources(): return blank.at[spot_x, spot_y, spot_z].add(rates * inside)  9.06 us
    gather x1, local copies, waits for them, and re-layouts, on_device(): nearby = final[spot_x, spot_y, spot_z] - well_data  8.9 us
    all_to_all x1, waiting for transfers between devices, from_everyone(): lax.all_to_all(jnp.broadcast_to(shard[None], (count, *shard.shape)), axis...  8.82 us
    unnamed x44, local copies, waits for them, and re-layouts  8.14 us
  transfers between devices with their start and end apart: 9, of which 1 were waited for; matrix products, arithmetic and copies ran while one was open for 15% of the time, Pallas kernels for 0%

commit v1 on v0

v1 whole, which is shorter than its diff:
```python
import functools
import math
import operator

import jax
import jax.numpy as jnp
from jax import lax
from jax.experimental import pallas as pl
from jax.experimental.pallas import tpu as pltpu
from jax.sharding import Mesh
from jax.sharding import PartitionSpec as P

FAR = "gx_0"
GX = ("gx_0", "gx_1")
GY = "gy"
ENS_GX = ("ens", "gx_0", "gx_1")

time_step = 0.2
head_slope = 0.5
molecular = 0.05
dispersivity = 0.1

RIM = 3
ROW = 8

VMEM_WHOLE = pl.BlockSpec(memory_space=pltpu.VMEM)
SMEM_WHOLE = pl.BlockSpec(memory_space=pltpu.SMEM)


def split(value, size):
    if size & (size - 1) == 0:
        return value >> (size.bit_length() - 1), value & (size - 1)
    return lax.div(value, jnp.int32(size)), lax.rem(value, jnp.int32(size))


def place_in(axes):
    position = lax.axis_index(axes)
    return position, position % 2 == 0


def up(field, axis):
    return pltpu.roll(field, field.shape[axis] - 1, axis)


def down(field, axis):
    return pltpu.roll(field, 1, axis)


def lane_mask(shape):
    lane = lax.broadcasted_iota(jnp.int32, shape, 1)
    return jnp.where(lane < shape[1] - 1, jnp.float32(time_step), jnp.float32(0.0))


def row_mask(shape, first, total):
    position = lax.broadcasted_iota(jnp.int32, shape, 0) - ROW + first
    is_open = (position >= 0) & (position + 1 < total)
    return jnp.where(is_open, jnp.float32(time_step), jnp.float32(0.0))


def plane_mask(plane, first, total):
    position = first - RIM + plane
    is_open = (position >= 0) & (position + 1 < total)
    return jnp.where(is_open, jnp.float32(time_step), jnp.float32(0.0))


def visit(count, hit, act):
    group = math.gcd(count, 8)

    def one(base, inner):
        @pl.when(hit(base + inner))
        def _():
            act(base + inner)

    def step(index, carry):
        base = index * group
        anyone = functools.reduce(operator.or_, [hit(base + k) for k in range(group)])

        @pl.when(anyone)
        def _():
            lax.fori_loop(0, group, lambda k, c: (one(base, k), c)[1], 0)

        return carry

    lax.fori_loop(0, count // group, step, 0)


def pack_x_kernel(start_ref, cond_ref, one_ref, two_ref):
    size = start_ref.shape[0]
    _, even = place_in(GX)
    first = jnp.where(even, 0, size - RIM)
    second = size - RIM - first
    for k in range(RIM):
        one_ref[0, k] = start_ref[first + k]
        one_ref[1, k] = cond_ref[first + k]
        two_ref[0, k] = start_ref[second + k]
        two_ref[1, k] = cond_ref[second + k]


def pack_y_kernel(start_ref, cond_ref, x_one_ref, x_two_ref, one_ref, two_ref):
    size, rows = start_ref.shape[:2]
    _, even = place_in(GY)

    def fill(low_ref, high_ref):
        for out_ref, begin in ((low_ref, 0), (high_ref, rows - RIM)):
            span = slice(begin, begin + RIM)
            for which, own_ref in ((0, start_ref), (1, cond_ref)):
                out_ref[which, 0:RIM] = x_one_ref[which, :, span, :]
                out_ref[which, RIM : RIM + size] = own_ref[:, span, :]
                out_ref[which, RIM + size :] = x_two_ref[which, :, span, :]

    @pl.when(even)
    def _():
        fill(one_ref, two_ref)

    @pl.when(jnp.logical_not(even))
    def _():
        fill(two_ref, one_ref)


def pack_seed_kernel(seed_ref, x_one_ref, x_two_ref, one_ref, two_ref):
    size, rows = seed_ref.shape[:2]
    rim = RIM - 1
    _, even = place_in(GY)

    def fill(low_ref, high_ref):
        for out_ref, begin in ((low_ref, 0), (high_ref, rows - rim)):
            span = slice(begin, begin + rim)
            out_ref[0:rim] = x_one_ref[:, span, :]
            out_ref[rim : rim + size] = seed_ref[:, span, :]
            out_ref[rim + size :] = x_two_ref[:, span, :]

    @pl.when(even)
    def _():
        fill(one_ref, two_ref)

    @pl.when(jnp.logical_not(even))
    def _():
        fill(two_ref, one_ref)


def spread(wide_ref, rim, own, x_one, x_two, y_one, y_two):
    size, rows = own.shape
    shift = RIM - rim
    _, even_x = place_in(GX)
    _, even_y = place_in(GY)
    base_one = jnp.where(even_x, shift, RIM + size)
    base_two = shift + RIM + size - base_one

    def copy_own(k, carry):
        wide_ref[RIM + k, ROW : ROW + rows] = own(k)
        return carry

    lax.fori_loop(0, size, copy_own, 0)
    for k in range(rim):
        wide_ref[base_one + k, ROW : ROW + rows] = x_one(k)
        wide_ref[base_two + k, ROW : ROW + rows] = x_two(k)

    def edges(low, high):
        for k in range(size + 2 * rim):
            if k < rim:
                plane = base_one + k
            elif k < rim + size:
                plane = shift + k
            else:
                plane = base_two + k - rim - size
            wide_ref[plane, ROW - rim : ROW] = low(k)
            wide_ref[plane, ROW + rows : ROW + rows + rim] = high(k)

    @pl.when(even_y)
    def _():
        edges(y_one, y_two)

    @pl.when(jnp.logical_not(even_y))
    def _():
        edges(y_two, y_one)


class Own:
    def __init__(self, shape, read):
        self.shape = shape
        self.read = read

    def __call__(self, k):
        return self.read(k)


def forward_kernel(
    grid_x,
    grid_y,
    source_cells,
    first_rates,
    second_rates,
    well_cells,
    well_data,
    well_weight,
    start_ref,
    cond_ref,
    x_one_ref,
    x_two_ref,
    y_one_ref,
    y_two_ref,
    survey_ref,
    weight_ref,
    root_ref,
    state_ref,
    next_ref,
    final_ref,
    seed_ref,
    edge_one_ref,
    edge_two_ref,
    partial_ref,
    row_ref,
    flux_ref,
):
    size, rows, depth = start_ref.shape
    wide = (root_ref.shape[1], depth)
    place_x, even_x = place_in(GX)
    place_y, _ = place_in(GY)
    anchor_x = place_x * size
    anchor_y = place_y * rows

    spread(
        state_ref,
        RIM,
        Own((size, rows), lambda k: start_ref[k]),
        lambda k: x_one_ref[0, k],
        lambda k: x_two_ref[0, k],
        lambda k: y_one_ref[0, k],
        lambda k: y_two_ref[0, k],
    )
    spread(
        root_ref,
        RIM,
        Own((size, rows), lambda k: jnp.exp(0.5 * cond_ref[k])),
        lambda k: jnp.exp(0.5 * x_one_ref[1, k]),
        lambda k: jnp.exp(0.5 * x_two_ref[1, k]),
        lambda k: jnp.exp(0.5 * y_one_ref[1, k]),
        lambda k: jnp.exp(0.5 * y_two_ref[1, k]),
    )
    row_ref[...] = row_mask(wide, anchor_y, grid_y)
    open_z = lane_mask(wide)

    def along_x(ref, plane):
        here = ref[plane]
        ahead = ref[plane + 1]
        cond = root_ref[plane] * root_ref[plane + 1]
        flux = head_slope * cond * here - (molecular + dispersivity * cond) * (ahead - here)
        return flux * plane_mask(plane, anchor_x, grid_x)

    def advanced(ref, plane):
        here = ref[plane]
        root = root_ref[plane]
        flux_x = along_x(ref, plane)
        cond_y = root * up(root, 0)
        flux_y = (row_ref[...] * (molecular + dispersivity * cond_y)) * (here - up(here, 0))
        cond_z = root * up(root, 1)
        flux_z = (open_z * (molecular + dispersivity * cond_z)) * (here - up(here, 1))
        change = (flux_x - flux_ref[...]) + (flux_y - down(flux_y, 0)) + (flux_z - down(flux_z, 1))
        flux_ref[...] = flux_x
        return here - change

    def spot(cell):
        line, along_z = split(cell, depth)
        along_x_, along_y = split(line, grid_y)
        return along_x_ - anchor_x, along_y - anchor_y, along_z

    def within(cell, rim):
        at_x, at_y, _ = spot(cell)
        return (at_x >= -rim) & (at_x < size + rim) & (at_y >= -rim) & (at_y < rows + rim)

    lane = lax.broadcasted_iota(jnp.int32, (1, depth), 1)

    flux_ref[...] = along_x(state_ref, 0)

    def first_step(plane, carry):
        next_ref[plane] = advanced(state_ref, plane)
        return carry

    lax.fori_loop(1, size + 2 * RIM - 1, first_step, 0)

    def add_first(index):
        at_x, at_y, at_z = spot(source_cells[index])
        where = (at_x + RIM, pl.ds(at_y + ROW, 1), slice(None))
        amount = time_step * first_rates[index]
        next_ref[where] = next_ref[where] + jnp.where(lane == at_z, amount, 0.0)

    visit(source_cells.shape[0], lambda i: within(source_cells[i], RIM - 1), add_first)

    flux_ref[...] = along_x(next_ref, RIM - 1)

    def second_step(k, carry):
        final_ref[k] = advanced(next_ref, k + RIM)[ROW : ROW + rows]
        return carry

    lax.fori_loop(0, size, second_step, 0)

    def add_second(index):
        at_x, at_y, at_z = spot(source_cells[index])
        where = (at_x, pl.ds(at_y, 1), slice(None))
        amount = time_step * second_rates[index]
        final_ref[where] = final_ref[where] + jnp.where(lane == at_z, amount, 0.0)

    visit(source_cells.shape[0], lambda i: within(source_cells[i], 0), add_second)

    partial_ref[...] = jnp.zeros((1, depth), jnp.float32)

    def compare(k, total):
        missed = final_ref[k] - survey_ref[k]
        seed = weight_ref[k] * missed
        seed_ref[k] = seed
        return total + jnp.sum((seed * missed).reshape(rows // 8, 8, depth), axis=0)

    total = lax.fori_loop(0, size, compare, jnp.zeros((8, depth), jnp.float32))
    partial_ref[...] = jnp.sum(total, axis=0, keepdims=True)

    def observe(index):
        at_x, at_y, at_z = spot(well_cells[index])
        where = (at_x, pl.ds(at_y, 1), slice(None))
        nearby = final_ref[where] - well_data[index]
        pull = jnp.where(lane == at_z, well_weight[index] * nearby, 0.0)
        seed_ref[where] = seed_ref[where] + pull
        partial_ref[...] = partial_ref[...] + pull * nearby

    visit(well_cells.shape[0], lambda i: within(well_cells[i], 0), observe)

    rim = RIM - 1
    first = jnp.where(even_x, 0, size - rim)
    second = size - rim - first
    for k in range(rim):
        edge_one_ref[k] = seed_ref[first + k]
        edge_two_ref[k] = seed_ref[second + k]


def adjoint_kernel(
    grid_x,
    grid_y,
    root_ref,
    state_ref,
    next_ref,
    seed_ref,
    x_one_ref,
    x_two_ref,
    y_one_ref,
    y_two_ref,
    grad_ref,
    back_ref,
    last_ref,
    middle_ref,
    partial_ref,
    row_ref,
    pull_ref,
    sens_ref,
):
    size, rows, depth = seed_ref.shape
    wide = (root_ref.shape[1], depth)
    place_x, _ = place_in(GX)
    place_y, _ = place_in(GY)
    anchor_x = place_x * size
    anchor_y = place_y * rows
    spread(
        last_ref,
        RIM - 1,
        Own((size, rows), lambda k: seed_ref[k]),
        lambda k: x_one_ref[k],
        lambda k: x_two_ref[k],
        lambda k: y_one_ref[k],
        lambda k: y_two_ref[k],
    )
    row_ref[...] = row_mask(wide, anchor_y, grid_y)
    open_z = lane_mask(wide)

    def along_x(adjoint_ref, tracer_ref, plane):
        jump = plane_mask(plane, anchor_x, grid_x) * (adjoint_ref[plane + 1] - adjoint_ref[plane])
        cond = root_ref[plane] * root_ref[plane + 1]
        pull = jump * (molecular + dispersivity * cond)
        push = jump * (head_slope * cond) + pull
        here = tracer_ref[plane]
        rise = head_slope * here - dispersivity * (tracer_ref[plane + 1] - here)
        return push, pull, jump * rise * (0.5 * cond)

    def along(adjoint, tracer, root, is_open, axis):
        jump = is_open * (up(adjoint, axis) - adjoint)
        cond = root * up(root, axis)
        pull = jump * (molecular + dispersivity * cond)
        sens = (jump * (tracer - up(tracer, axis))) * ((0.5 * dispersivity) * cond)
        return pull - down(pull, axis), sens + down(sens, axis)

    def reversed_step(adjoint_ref, tracer_ref, plane):
        push, pull, sens = along_x(adjoint_ref, tracer_ref, plane)
        adjoint = adjoint_ref[plane]
        tracer = tracer_ref[plane]
        root = root_ref[plane]
        change_y, sens_y = along(adjoint, tracer, root, row_ref[...], 0)
        change_z, sens_z = along(adjoint, tracer, root, open_z, 1)
        updated = adjoint + (push - pull_ref[...]) + change_y + change_z
        gradient = (sens + sens_ref[...]) + sens_y + sens_z
        pull_ref[...] = pull
        sens_ref[...] = sens
        return updated, gradient

    def begin(adjoint_ref, tracer_ref, plane):
        _, pull, sens = along_x(adjoint_ref, tracer_ref, plane)
        pull_ref[...] = pull
        sens_ref[...] = sens

    begin(last_ref, next_ref, RIM - 2)

    def later(plane, carry):
        updated, gradient = reversed_step(last_ref, next_ref, plane)
        middle_ref[plane] = updated
        partial_ref[plane] = gradient
        return carry

    lax.fori_loop(RIM - 1, size + RIM + 1, later, 0)

    begin(middle_ref, state_ref, RIM - 1)

    def earlier(k, carry):
        updated, gradient = reversed_step(middle_ref, state_ref, k + RIM)
        back_ref[k] = updated[ROW : ROW + rows]
        grad_ref[k] = (gradient + partial_ref[k + RIM])[ROW : ROW + rows]
        return carry

    lax.fori_loop(0, size, earlier, 0)


def call(kernel, outs, operands, *, smem=0, scratch=(), flops=1_000_000, limit=2, name):
    shapes = tuple(
        pltpu.VMEM(shape, jnp.float32) if kept else jax.ShapeDtypeStruct(shape, jnp.float32)
        for shape, kept in outs
    )
    operands = operands[:smem] + tuple(
        pltpu.with_memory_space_constraint(operand, pltpu.VMEM) for operand in operands[smem:]
    )
    return pl.pallas_call(
        kernel,
        out_shape=shapes,
        in_specs=[SMEM_WHOLE] * smem + [VMEM_WHOLE] * (len(operands) - smem),
        out_specs=tuple(VMEM_WHOLE for _ in outs),
        scratch_shapes=[pltpu.VMEM(shape, jnp.float32) for shape in scratch],
        cost_estimate=pl.CostEstimate(flops=flops, transcendentals=0, bytes_accessed=1_000_000),
        compiler_params=pltpu.CompilerParams(vmem_limit_bytes=limit << 20),
        name=name,
    )(*operands)


def swapped(one, two, axes):
    count = lax.axis_size(axes)
    outer = [(i, i + 1) for i in range(1, count - 1, 2)]
    inner = [(i, i + 1) for i in range(0, count - 1, 2)]
    back = lambda pairs: pairs + [(b, a) for a, b in pairs]
    return lax.ppermute(one, axes, back(outer)), lax.ppermute(two, axes, back(inner))


def from_everyone(shard, axis):
    count = lax.axis_size(axis)
    return lax.all_to_all(
        jnp.broadcast_to(shard[None], (count, *shard.shape)), axis, 0, 0, tiled=True
    )


def on_device(
    log_cond,
    checkpoint,
    survey,
    survey_weight,
    well_cells,
    well_data,
    well_weight,
    source_cells,
    source_rate,
    step_number,
):
    size, rows, depth = checkpoint.shape
    grid_x = size * lax.axis_size(GX)
    grid_y = rows * lax.axis_size(GY)
    clock = step_number.astype(jnp.float32)[0]
    first_rates = source_rate * (1.0 + 0.5 * jnp.sin(0.05 * clock))
    second_rates = source_rate * (1.0 + 0.5 * jnp.sin(0.05 * (clock + 1.0)))

    planes = size + 2 * RIM
    wide = (planes, rows + 2 * ROW, depth)
    flat = wide[1:]
    block = (size, rows, depth)
    rim = RIM - 1

    x_edge = (2, RIM, rows, depth)
    x_one, x_two = call(pack_x_kernel, ((x_edge, True),) * 2, (checkpoint, log_cond), name="pack_x")
    x_one, x_two = swapped(x_one, x_two, GX)
    y_edge = (2, planes, RIM, depth)
    y_one, y_two = call(
        pack_y_kernel, ((y_edge, True),) * 2, (checkpoint, log_cond, x_one, x_two), name="pack_y"
    )
    y_one, y_two = swapped(y_one, y_two, GY)

    s_edge = (rim, rows, depth)
    root, state, later, final, seed, s_one, s_two, partial = call(
        functools.partial(forward_kernel, grid_x, grid_y),
        (
            (wide, True),
            (wide, True),
            (wide, True),
            (block, False),
            (block, True),
            (s_edge, True),
            (s_edge, True),
            ((1, depth), True),
        ),
        (
            source_cells,
            first_rates,
            second_rates,
            well_cells,
            well_data,
            well_weight,
            checkpoint,
            log_cond,
            x_one,
            x_two,
            y_one,
            y_two,
            survey,
            survey_weight,
        ),
        smem=6,
        scratch=(flat, flat),
        flops=20_000_000,
        limit=6,
        name="forward",
    )

    s_one, s_two = swapped(s_one, s_two, GX)
    t_edge = (size + 2 * rim, rim, depth)
    t_one, t_two = call(pack_seed_kernel, ((t_edge, True),) * 2, (seed, s_one, s_two), name="pack_seed")
    t_one, t_two = swapped(t_one, t_two, GY)
    grad, back = call(
        functools.partial(adjoint_kernel, grid_x, grid_y),
        ((block, False), (block, False)),
        (root, state, later, seed, s_one, s_two, t_one, t_two),
        scratch=(wide, wide, wide, flat, flat, flat),
        flops=20_000_000,
        limit=12,
        name="adjoint",
    )

    near = jnp.sum(from_everyone(partial, ("gx_1", GY)), axis=0)
    total = jnp.sum(from_everyone(near, FAR))
    misfit = (0.5 * total / (grid_x * grid_y * depth)).reshape(1)
    return (grad, back, final, misfit)


def solution(mesh):
    ens, along_x, along_y = (mesh.shape[name] for name in ("ens", "gx", "gy"))
    finer = Mesh(
        mesh.devices.reshape(ens, along_x // 2, 2, along_y), ("ens", "gx_0", "gx_1", "gy")
    )
    field = P(ENS_GX, "gy", None)
    return jax.shard_map(
        on_device,
        mesh=finer,
        in_specs=(field,) * 4 + (P("ens"),) * 6,
        out_specs=(field, field, field, P("ens")),
        check_vma=False,
    )
```

time: 175 us -> 124 us (0.71)
  other arithmetic: 49.9 us -> 0.62 us
  local copies, waits for them, and re-layouts: 30.7 us -> 6.23 us
  Pallas kernels: 0 us -> 13.9 us
  waiting for transfers between devices: 8.84 us -> 18.5 us
  starting transfers between devices: 67.3 us -> 72.2 us
  blocking collectives: 12.4 us -> 8.61 us
    scatter-add x3 -> x0, other arithmetic: 24.5 us -> none  [the longest x1 15.4 us: on_device(): seed = seed.at[spot_x, spot_y, spot_z].add(well_weight * nearby * owned)]
    pallas_call x0 -> x5, Pallas kernels: none -> 13.9 us  [call(): pl.pallas_call(kernel, out_shape=shapes, in_specs=[SMEM_WHOLE] * smem + [...]
    slice x33 -> x0, local copies, waits for them, and re-layouts: 10.5 us -> none  [the longest x4 2.96 us: adjoint_step(): push_x[1:] + pull_x[:-1]]
    mul x21 -> x1, other arithmetic: 10.4 us -> 0.01 us  [on_device(): second_rates = source_rate * (1.0 + 0.5 * jnp.sin(0.05 * (clock + 1.0)))]
    gather x1 -> x0, local copies, waits for them, and re-layouts: 8.9 us -> none  [on_device(): nearby = final[spot_x, spot_y, spot_z] - well_data]
    all_to_all x1, waiting for transfers between devices: 8.82 us -> 16.5 us  [from_everyone(): lax.all_to_all(jnp.broadcast_to(shard[None], (count, *shard.shape)), axis...]
    add x5 -> x0, other arithmetic: 5.83 us -> none  [the longest x2 2.34 us: adjoint_step(): updated = updated + (push_z[:, :, 1:] + pull_z[:, :, :-1])[1:-1, 1:-1]]
    ppermute x8, starting transfers between devices: 21.7 us -> 27 us  [the longest x4 24.2 us: swapped(): lax.ppermute(two, axes, back(inner))]
  transfers between devices with their start and end apart: 9 -> 9, of which waited for: 1 -> 3; matrix products, arithmetic and copies ran while one was open for 15% -> 1% of each run, Pallas kernels for 0% -> 0%
where the time goes in v1:
time: 124 us
  starting transfers between devices  72.2 us (58%)
  waiting for transfers between devices  18.5 us (15%)
  Pallas kernels  13.9 us (11%)
  blocking collectives  8.61 us (7%)
  local copies, waits for them, and re-layouts  6.23 us (5%)
  between operations  3.43 us (3%)
    all_to_all x1, starting transfers between devices, from_everyone(): lax.all_to_all(jnp.broadcast_to(shard[None], (count, *shard.shape)), axis...  45.3 us
    ppermute x4, starting transfers between devices, swapped(): lax.ppermute(two, axes, back(inner))  24.2 us
    all_to_all x1, waiting for transfers between devices, from_everyone(): lax.all_to_all(jnp.broadcast_to(shard[None], (count, *shard.shape)), axis...  16.5 us
    pallas_call x5, Pallas kernels, call(): pl.pallas_call(kernel, out_shape=shapes, in_specs=[SMEM_WHOLE] * smem + [...  13.9 us
    all_to_all x1, blocking collectives, from_everyone(): lax.all_to_all(jnp.broadcast_to(shard[None], (count, *shard.shape)), axis...  8.61 us
    unnamed x26, local copies, waits for them, and re-layouts  5.61 us
    ppermute x4, starting transfers between devices, swapped(): lax.ppermute(one, axes, back(outer))  2.8 us
  transfers between devices with their start and end apart: 9, of which 3 were waited for; matrix products, arithmetic and copies ran while one was open for 1% of the time, Pallas kernels for 0%

profile of v1, /device:TPU:40, one launch (start us, length us, event | category | flops | bytes accessed | tf_op | source)
XLA Modules:
  0.0 123.5 jit_solution(4347607211374031059)
XLA Ops:
  0.6 0.0 copy-start
  0.6 1.0 copy-done
  1.7 0.0 copy-start.2
  1.7 1.0 copy-done.2
  2.7 0.0 copy-start.1
  2.7 0.1 pack_x.1
  2.8 0.8 collective-permute-start
  3.6 6.1 %collective-permute-start.1 = (f32[2,3,128,128]{3,2,1,0:T(8,128)S(1)}, f32[2,3,128,128]{3,2,1,0:T(8,128)S(1)}, u32[]{:S(2)}, u32[]{:S(2)}) collective-permute-start(f32[2,3,128,128]{3,2,1,0:T(8,128)S(1)} %get-tuple-element.21), channel_id=1, source_target_pairs={{0,4},{8,12},{16,20},{24,28},{32,36},{40,44},{48,52},{56,60},{64,6... | collective-permute-start | bytes 1179656 | tf_op jit(solution)/shard_map/ppermute | solution.py:452
  10.5 0.0 copy-start.6
  10.5 0.0 copy-start.7
  10.5 0.0 collective-permute-done.x_one_ref
  10.5 0.5 collective-permute-done.1.x_two_ref
  11.0 0.0 copy-done.1
  11.0 0.0 copy-done.3
  11.0 0.0 copy-start.9
  11.0 0.0 copy-start.10
  11.1 0.7 collective-permute-start.2
  11.8 6.5 %collective-permute-start.3 = (f32[2,14,3,128]{3,2,1,0:T(4,128)S(1)}, f32[2,14,3,128]{3,2,1,0:T(4,128)S(1)}, u32[]{:S(2)}, u32[]{:S(2)}) collective-permute-start(f32[2,14,3,128]{3,2,1,0:T(4,128)S(1)} %get-tuple-element.23), channel_id=1, source_target_pairs={{0,1},{2,3},{1,0},{3,2},{4,5},{6,7},{5,4},{7,6},{8,9},{10,11},{9,8... | collective-permute-start | bytes 129032 | tf_op jit(solution)/shard_map/ppermute | solution.py:452
  18.2 0.0 copy-start.12
  18.2 0.6 copy-done.12
  18.9 0.0 collective-permute-done.2.y_one_ref
  18.9 1.5 %collective-permute-done.3.y_two_ref = f32[2,14,3,128]{3,2,1,0:T(4,128)S(1)} collective-permute-done((f32[2,14,3,128]{3,2,1,0:T(4,128)S(1)}, f32[2,14,3,128]{3,2,1,0:T(4,128)S(1)}, u32[]{:S(2)}, u32[]{:S(2)}) %collective-permute-start.3) | collective-permute-done | bytes 43040 | tf_op jit(solution)/shard_map/ppermute | solution.py:452
  20.4 0.0 copy-start.8
  20.4 0.0 copy-start.11
  20.4 0.0 copy-done.6
  20.4 0.0 copy-done.7
  20.4 0.0 copy-done.9
  20.4 0.0 copy-done.10
  20.4 0.6 copy-done.8
  21.1 0.0 copy-done.11
  21.1 8.7 %forward.1 = (f32[14,144,128]{2,1,0:T(8,128)S(1)}, f32[14,144,128]{2,1,0:T(8,128)S(1)}, f32[14,144,128]{2,1,0:T(8,128)S(1)}, f32[8,128,128]{2,1,0:T(8,128)}, f32...) custom-call(s32[64]{0:T(128)S(1)} %copy-done.11, ...), custom_call_target="tpu_custom_call" | custom-call | flops 20000000 | bytes 1000000 | tf_op jit(solution)/shard_map/forward/pallas_call | solution.py:435
  29.7 1.0 copy-done.4
  30.7 0.7 collective-permute-start.4
  31.4 7.3 %collective-permute-start.5 = (f32[2,128,128]{2,1,0:T(8,128)S(1)}, f32[2,128,128]{2,1,0:T(8,128)S(1)}, u32[]{:S(2)}, u32[]{:S(2)}) collective-permute-start(f32[2,128,128]{2,1,0:T(8,128)S(1)} %get-tuple-element.29), channel_id=1, source_target_pairs={{0,4},{8,12},{16,20},{24,28},{32,36},{40,44},{48,52},{56,60},{64,6... | collective-permute-start | bytes 393224 | tf_op jit(solution)/shard_map/ppermute | solution.py:452
  38.7 8.6 %all_to_all.10 = f32[8,1,128]{2,1,0:T(1,128)S(1)} all-to-all(f32[8,1,128]{2,1,0:T(1,128)S(1)} %broadcast_in_dim.7), channel_id=1, replica_groups=mesh['ens'=2,'gx_0'=32,'gx_1'=2,'gy'=4] {'gx_1','gy'}, dimensions={0} | all-to-all | bytes 8192 | tf_op jit(solution)/shard_map/all_to_all | solution.py:457
  47.3 0.6 broadcast_in_dim.16
  47.9 45.3 %all-to-all-start.1 = ((f32[32,1,128]{2,1,0:T(1,128)}), f32[32,1,128]{2,1,0:T(1,128)S(1)}, u32[]{:S(2)}, u32[]{:S(2)}) async-start(f32[32,1,128]{2,1,0:T(1,128)} %broadcast_in_dim.16), calls=%async_computation.1 | async-start | bytes 32768 | tf_op jit(solution)/shard_map/all_to_all | solution.py:457
  93.2 0.0 collective-permute-done.4.x_one_ref
  93.2 0.0 collective-permute-done.5.x_two_ref
  93.2 0.7 collective-permute-start.6
  93.9 4.3 %collective-permute-start.7 = (f32[12,2,128]{2,1,0:T(2,128)S(1)}, f32[12,2,128]{2,1,0:T(2,128)S(1)}, u32[]{:S(2)}, u32[]{:S(2)}) collective-permute-start(f32[12,2,128]{2,1,0:T(2,128)S(1)} %get-tuple-element.31), channel_id=1, source_target_pairs={{0,1},{2,3},{1,0},{3,2},{4,5},{6,7},{5,4},{7,6},{8,9},{10,11},{9,8... | collective-permute-start | bytes 36872 | tf_op jit(solution)/shard_map/ppermute | solution.py:452
  98.3 16.5 %all-to-all-done.1 = f32[32,1,128]{2,1,0:T(1,128)S(1)} async-done(((f32[32,1,128]{2,1,0:T(1,128)}), f32[32,1,128]{2,1,0:T(1,128)S(1)}, u32[]{:S(2)}, u32[]{:S(2)}) %all-to-all-start.1) | async-done | bytes 16416 | tf_op jit(solution)/shard_map/all_to_all | solution.py:457
  114.8 0.6 reduce_sum.19
  116.0 0.0 collective-permute-done.6.y_one_ref
  116.1 0.0 collective-permute-done.7.y_two_ref
  116.1 0.0 copy-start.5
  116.1 1.2 copy-done.5
  117.3 5.1 %adjoint.1 = (f32[8,128,128]{2,1,0:T(8,128)}, f32[8,128,128]{2,1,0:T(8,128)}) custom-call(f32[14,144,128]{2,1,0:T(8,128)S(1)} %get-tuple-element.24.root_ref, f32[14,144,128]{2,1,0:T(8,128)S(1)} %get-tuple-element.25.state_ref, f32[14,144,128]{2,1,0:T(8,128)S(1)} %copy-done.5, f32[8,128,128]{2,1,0:T(8,128)S(1)} %get-tuple-element.27.seed_ref, ...), custom_call_target="tpu_custom_call" | custom-call | flops 20000000 | bytes 1000000 | tf_op jit(solution)/shard_map/adjoint/pallas_call | solution.py:435
  (7 shorter events, 0.1 us)
Async XLA Ops:
  0.6 1.0 copy-start
  1.7 1.0 copy-start.2
  2.7 8.3 %copy-start.1 = (f32[8,128,128]{2,1,0:T(8,128)S(1)}, f32[8,128,128]{2,1,0:T(8,128)}, u32[]{:S(2)}) copy-start(f32[8,128,128]{2,1,0:T(8,128)} %start_ref.5) | copy-start | bytes 1572868
  2.7 8.3 %copy-start.3 = (f32[8,128,128]{2,1,0:T(8,128)S(1)}, f32[8,128,128]{2,1,0:T(8,128)}, u32[]{:S(2)}) copy-start(f32[8,128,128]{2,1,0:T(8,128)} %cond_ref.5) | copy-start | bytes 1572868
  2.8 7.8 %collective-permute-start = (f32[2,3,128,128]{3,2,1,0:T(8,128)S(1)}, f32[2,3,128,128]{3,2,1,0:T(8,128)S(1)}, u32[]{:S(2)}, u32[]{:S(2)}) collective-permute-start(f32[2,3,128,128]{3,2,1,0:T(8,128)S(1)} %get-tuple-element.20), channel_id=1, source_target_pairs={{4,8},{12,16},{20,24},{28,32},{36,40},{44,48},{52,56},{60,64},{68,... | collective-permute-start | bytes 1179656 | tf_op jit(solution)/shard_map/ppermute | solution.py:452
  3.6 7.4 %collective-permute-start.1 = (f32[2,3,128,128]{3,2,1,0:T(8,128)S(1)}, f32[2,3,128,128]{3,2,1,0:T(8,128)S(1)}, u32[]{:S(2)}, u32[]{:S(2)}) collective-permute-start(f32[2,3,128,128]{3,2,1,0:T(8,128)S(1)} %get-tuple-element.21), channel_id=1, source_target_pairs={{0,4},{8,12},{16,20},{24,28},{32,36},{40,44},{48,52},{56,60},{64,6... | collective-permute-start | bytes 1179656 | tf_op jit(solution)/shard_map/ppermute | solution.py:452
  10.5 9.9 %copy-start.6 = (f32[8,128,128]{2,1,0:T(8,128)S(1)}, f32[8,128,128]{2,1,0:T(8,128)}, u32[]{:S(2)}) copy-start(f32[8,128,128]{2,1,0:T(8,128)} %survey_ref.1) | copy-start | bytes 1572868
  10.5 9.9 %copy-start.7 = (f32[8,128,128]{2,1,0:T(8,128)S(1)}, f32[8,128,128]{2,1,0:T(8,128)}, u32[]{:S(2)}) copy-start(f32[8,128,128]{2,1,0:T(8,128)} %weight_ref.1) | copy-start | bytes 1572868
  11.0 9.4 %copy-start.9 = (f32[256]{0:T(256)S(1)}, f32[256]{0:T(256)}, u32[]{:S(2)}) copy-start(f32[256]{0:T(256)} %well_data.1) | copy-start | bytes 3076
  11.0 9.4 %copy-start.10 = (f32[256]{0:T(256)S(1)}, f32[256]{0:T(256)}, u32[]{:S(2)}) copy-start(f32[256]{0:T(256)} %well_weight.1) | copy-start | bytes 3076
  11.1 7.8 %collective-permute-start.2 = (f32[2,14,3,128]{3,2,1,0:T(4,128)S(1)}, f32[2,14,3,128]{3,2,1,0:T(4,128)S(1)}, u32[]{:S(2)}, u32[]{:S(2)}) collective-permute-start(f32[2,14,3,128]{3,2,1,0:T(4,128)S(1)} %get-tuple-element.22), channel_id=1, source_target_pairs={{1,2},{2,1},{5,6},{6,5},{9,10},{10,9},{13,14},{14,13},{17,18},{18,... | collective-permute-start | bytes 129032 | tf_op jit(solution)/shard_map/ppermute | solution.py:452
  11.8 8.6 %collective-permute-start.3 = (f32[2,14,3,128]{3,2,1,0:T(4,128)S(1)}, f32[2,14,3,128]{3,2,1,0:T(4,128)S(1)}, u32[]{:S(2)}, u32[]{:S(2)}) collective-permute-start(f32[2,14,3,128]{3,2,1,0:T(4,128)S(1)} %get-tuple-element.23), channel_id=1, source_target_pairs={{0,1},{2,3},{1,0},{3,2},{4,5},{6,7},{5,4},{7,6},{8,9},{10,11},{9,8... | collective-permute-start | bytes 129032 | tf_op jit(solution)/shard_map/ppermute | solution.py:452
  18.2 0.7 copy-start.12
  20.4 0.7 copy-start.8
  20.4 0.7 copy-start.11
  29.7 1.0 copy-start.4
  30.7 62.5 %collective-permute-start.4 = (f32[2,128,128]{2,1,0:T(8,128)S(1)}, f32[2,128,128]{2,1,0:T(8,128)S(1)}, u32[]{:S(2)}, u32[]{:S(2)}) collective-permute-start(f32[2,128,128]{2,1,0:T(8,128)S(1)} %get-tuple-element.28), channel_id=1, source_target_pairs={{4,8},{12,16},{20,24},{28,32},{36,40},{44,48},{52,56},{60,64},{68,... | collective-permute-start | bytes 393224 | tf_op jit(solution)/shard_map/ppermute | solution.py:452
  31.4 61.8 %collective-permute-start.5 = (f32[2,128,128]{2,1,0:T(8,128)S(1)}, f32[2,128,128]{2,1,0:T(8,128)S(1)}, u32[]{:S(2)}, u32[]{:S(2)}) collective-permute-start(f32[2,128,128]{2,1,0:T(8,128)S(1)} %get-tuple-element.29), channel_id=1, source_target_pairs={{0,4},{8,12},{16,20},{24,28},{32,36},{40,44},{48,52},{56,60},{64,6... | collective-permute-start | bytes 393224 | tf_op jit(solution)/shard_map/ppermute | solution.py:452
  47.9 66.9 %all-to-all-start.1 = ((f32[32,1,128]{2,1,0:T(1,128)}), f32[32,1,128]{2,1,0:T(1,128)S(1)}, u32[]{:S(2)}, u32[]{:S(2)}) async-start(f32[32,1,128]{2,1,0:T(1,128)} %broadcast_in_dim.16), calls=%async_computation.1 | async-start | bytes 32768 | tf_op jit(solution)/shard_map/all_to_all | solution.py:457
  93.2 22.8 %collective-permute-start.6 = (f32[12,2,128]{2,1,0:T(2,128)S(1)}, f32[12,2,128]{2,1,0:T(2,128)S(1)}, u32[]{:S(2)}, u32[]{:S(2)}) collective-permute-start(f32[12,2,128]{2,1,0:T(2,128)S(1)} %get-tuple-element.30), channel_id=1, source_target_pairs={{1,2},{2,1},{5,6},{6,5},{9,10},{10,9},{13,14},{14,13},{17,18},{18,... | collective-permute-start | bytes 36872 | tf_op jit(solution)/shard_map/ppermute | solution.py:452
  93.9 22.2 %collective-permute-start.7 = (f32[12,2,128]{2,1,0:T(2,128)S(1)}, f32[12,2,128]{2,1,0:T(2,128)S(1)}, u32[]{:S(2)}, u32[]{:S(2)}) collective-permute-start(f32[12,2,128]{2,1,0:T(2,128)S(1)} %get-tuple-element.31), channel_id=1, source_target_pairs={{0,1},{2,3},{1,0},{3,2},{4,5},{6,7},{5,4},{7,6},{8,9},{10,11},{9,8... | collective-permute-start | bytes 36872 | tf_op jit(solution)/shard_map/ppermute | solution.py:452
  116.1 1.2 copy-start.5

commit v2 on v1

--- a/solution.py
+++ b/solution.py
@@ -20,11 +20,8 @@
 molecular = 0.05
 dispersivity = 0.1
 
-RIM = 3
+RIM = 2
 ROW = 8
-
-VMEM_WHOLE = pl.BlockSpec(memory_space=pltpu.VMEM)
-SMEM_WHOLE = pl.BlockSpec(memory_space=pltpu.SMEM)
 
 
 def split(value, size):
@@ -84,16 +81,22 @@
     lax.fori_loop(0, count // group, step, 0)
 
 
-def pack_x_kernel(start_ref, cond_ref, one_ref, two_ref):
+def pack_x_kernel(start_ref, cond_ref, one_ref, two_ref, done):
     size = start_ref.shape[0]
     _, even = place_in(GX)
     first = jnp.where(even, 0, size - RIM)
     second = size - RIM - first
-    for k in range(RIM):
-        one_ref[0, k] = start_ref[first + k]
-        one_ref[1, k] = cond_ref[first + k]
-        two_ref[0, k] = start_ref[second + k]
-        two_ref[1, k] = cond_ref[second + k]
+    copies = []
+    for out_ref, begin in ((one_ref, first), (two_ref, second)):
+        for which, own_ref in ((0, start_ref), (1, cond_ref)):
+            source = own_ref.at[pl.ds(begin, RIM)]
+            copies.append(
+                pltpu.make_async_copy(source, out_ref.at[which], done.at[len(copies)])
+            )
+    for copy in copies:
+        copy.start()
+    for copy in copies:
+        copy.wait()
 
 
 def pack_y_kernel(start_ref, cond_ref, x_one_ref, x_two_ref, one_ref, two_ref):
@@ -119,7 +122,7 @@
 
 def pack_seed_kernel(seed_ref, x_one_ref, x_two_ref, one_ref, two_ref):
     size, rows = seed_ref.shape[:2]
-    rim = RIM - 1
+    rim = RIM
     _, even = place_in(GY)
 
     def fill(low_ref, high_ref):
@@ -187,12 +190,13 @@
 def forward_kernel(
     grid_x,
     grid_y,
-    source_cells,
-    first_rates,
-    second_rates,
-    well_cells,
-    well_data,
-    well_weight,
+    first_factor,
+    second_factor,
+    source_cells_ref,
+    source_rate_ref,
+    well_cells_ref,
+    well_data_ref,
+    well_weight_ref,
     start_ref,
     cond_ref,
     x_one_ref,
@@ -211,7 +215,26 @@
     partial_ref,
     row_ref,
     flux_ref,
+    source_cells,
+    source_rate,
+    well_cells,
+    well_data,
+    well_weight,
+    done,
 ):
+    lists = (
+        (source_cells_ref, source_cells),
+        (source_rate_ref, source_rate),
+        (well_cells_ref, well_cells),
+        (well_data_ref, well_data),
+        (well_weight_ref, well_weight),
+    )
+    copies = [
+        pltpu.make_async_copy(source, target, done.at[k])
+        for k, (source, target) in enumerate(lists)
+    ]
+    for copy in copies:
+        copy.start()
     size, rows, depth = start_ref.shape
     wide = (root_ref.shape[1], depth)
     place_x, even_x = place_in(GX)
@@ -278,10 +301,13 @@
 
     lax.fori_loop(1, size + 2 * RIM - 1, first_step, 0)
 
+    for copy in copies:
+        copy.wait()
+
     def add_first(index):
         at_x, at_y, at_z = spot(source_cells[index])
         where = (at_x + RIM, pl.ds(at_y + ROW, 1), slice(None))
-        amount = time_step * first_rates[index]
+        amount = time_step * (source_rate[index] * first_factor[0])
         next_ref[where] = next_ref[where] + jnp.where(lane == at_z, amount, 0.0)
 
     visit(source_cells.shape[0], lambda i: within(source_cells[i], RIM - 1), add_first)
@@ -297,7 +323,7 @@
     def add_second(index):
         at_x, at_y, at_z = spot(source_cells[index])
         where = (at_x, pl.ds(at_y, 1), slice(None))
-        amount = time_step * second_rates[index]
+        amount = time_step * (source_rate[index] * second_factor[0])
         final_ref[where] = final_ref[where] + jnp.where(lane == at_z, amount, 0.0)
 
     visit(source_cells.shape[0], lambda i: within(source_cells[i], 0), add_second)
@@ -323,10 +349,9 @@
 
     visit(well_cells.shape[0], lambda i: within(well_cells[i], 0), observe)
 
-    rim = RIM - 1
-    first = jnp.where(even_x, 0, size - rim)
-    second = size - rim - first
-    for k in range(rim):
+    first = jnp.where(even_x, 0, size - RIM)
+    second = size - RIM - first
+    for k in range(RIM):
         edge_one_ref[k] = seed_ref[first + k]
         edge_two_ref[k] = seed_ref[second + k]
 
@@ -359,7 +384,7 @@
     anchor_y = place_y * rows
     spread(
         last_ref,
-        RIM - 1,
+        RIM,
         Own((size, rows), lambda k: seed_ref[k]),
         lambda k: x_one_ref[k],
         lambda k: x_two_ref[k],
@@ -424,24 +449,28 @@
     lax.fori_loop(0, size, earlier, 0)
 
 
-def call(kernel, outs, operands, *, smem=0, scratch=(), flops=1_000_000, limit=2, name):
+def call(kernel, outs, operands, *, scratch=(), flops=1_000_000, limit=2):
     shapes = tuple(
-        pltpu.VMEM(shape, jnp.float32) if kept else jax.ShapeDtypeStruct(shape, jnp.float32)
-        for shape, kept in outs
-    )
-    operands = operands[:smem] + tuple(
-        pltpu.with_memory_space_constraint(operand, pltpu.VMEM) for operand in operands[smem:]
-    )
+        jax.ShapeDtypeStruct(shape, jnp.float32) if space is None else space(shape, jnp.float32)
+        for shape, space in outs
+    )
+    arrays = [
+        array if space == pltpu.SMEM else pltpu.with_memory_space_constraint(array, space)
+        for array, space in operands
+    ]
     return pl.pallas_call(
         kernel,
         out_shape=shapes,
-        in_specs=[SMEM_WHOLE] * smem + [VMEM_WHOLE] * (len(operands) - smem),
-        out_specs=tuple(VMEM_WHOLE for _ in outs),
-        scratch_shapes=[pltpu.VMEM(shape, jnp.float32) for shape in scratch],
+        in_specs=[pl.BlockSpec(memory_space=space) for _, space in operands],
+        out_specs=tuple(pl.BlockSpec(memory_space=pltpu.VMEM) for _ in outs),
+        scratch_shapes=scratch,
         cost_estimate=pl.CostEstimate(flops=flops, transcendentals=0, bytes_accessed=1_000_000),
         compiler_params=pltpu.CompilerParams(vmem_limit_bytes=limit << 20),
-        name=name,
-    )(*operands)
+    )(*arrays)
+
+
+def kept(*arrays, space=pltpu.VMEM):
+    return tuple((array, space) for array in arrays)
 
 
 def swapped(one, two, axes):
@@ -474,78 +503,65 @@
     size, rows, depth = checkpoint.shape
     grid_x = size * lax.axis_size(GX)
     grid_y = rows * lax.axis_size(GY)
-    clock = step_number.astype(jnp.float32)[0]
-    first_rates = source_rate * (1.0 + 0.5 * jnp.sin(0.05 * clock))
-    second_rates = source_rate * (1.0 + 0.5 * jnp.sin(0.05 * (clock + 1.0)))
+    clock = step_number.astype(jnp.float32)
+    first_factor = 1.0 + 0.5 * jnp.sin(0.05 * clock)
+    second_factor = 1.0 + 0.5 * jnp.sin(0.05 * (clock + 1.0))
 
     planes = size + 2 * RIM
     wide = (planes, rows + 2 * ROW, depth)
     flat = wide[1:]
     block = (size, rows, depth)
-    rim = RIM - 1
+    f32 = functools.partial(pltpu.VMEM, dtype=jnp.float32)
+    dma = pltpu.SemaphoreType.DMA
 
     x_edge = (2, RIM, rows, depth)
-    x_one, x_two = call(pack_x_kernel, ((x_edge, True),) * 2, (checkpoint, log_cond), name="pack_x")
+    x_one, x_two = call(
+        pack_x_kernel,
+        kept(x_edge, x_edge),
+        kept(checkpoint, log_cond, space=pltpu.HBM),
+        scratch=[dma((4,))],
+    )
     x_one, x_two = swapped(x_one, x_two, GX)
     y_edge = (2, planes, RIM, depth)
     y_one, y_two = call(
-        pack_y_kernel, ((y_edge, True),) * 2, (checkpoint, log_cond, x_one, x_two), name="pack_y"
+        pack_y_kernel, kept(y_edge, y_edge), kept(checkpoint, log_cond, x_one, x_two)
     )
     y_one, y_two = swapped(y_one, y_two, GY)
 
-    s_edge = (rim, rows, depth)
+    s_edge = (RIM, rows, depth)
+    lists = (source_cells, source_rate, well_cells, well_data, well_weight)
+    fields = (checkpoint, log_cond, x_one, x_two, y_one, y_two, survey, survey_weight)
     root, state, later, final, seed, s_one, s_two, partial = call(
         functools.partial(forward_kernel, grid_x, grid_y),
-        (
-            (wide, True),
-            (wide, True),
-            (wide, True),
-            (block, False),
-            (block, True),
-            (s_edge, True),
-            (s_edge, True),
-            ((1, depth), True),
-        ),
-        (
-            source_cells,
-            first_rates,
-            second_rates,
-            well_cells,
-            well_data,
-            well_weight,
-            checkpoint,
-            log_cond,
-            x_one,
-            x_two,
-            y_one,
-            y_two,
-            survey,
-            survey_weight,
-        ),
-        smem=6,
-        scratch=(flat, flat),
+        kept(wide, wide, wide)
+        + kept(block, space=None)
+        + kept(block, s_edge, s_edge, (1, depth)),
+        kept(first_factor, second_factor, space=pltpu.SMEM)
+        + kept(*lists, space=pltpu.HBM)
+        + kept(*fields),
+        scratch=[f32(flat), f32(flat)]
+        + [pltpu.SMEM(array.shape, array.dtype) for array in lists]
+        + [dma((len(lists),))],
         flops=20_000_000,
-        limit=6,
-        name="forward",
+        limit=4,
     )
 
     s_one, s_two = swapped(s_one, s_two, GX)
-    t_edge = (size + 2 * rim, rim, depth)
-    t_one, t_two = call(pack_seed_kernel, ((t_edge, True),) * 2, (seed, s_one, s_two), name="pack_seed")
+    t_edge = (planes, RIM, depth)
+    t_one, t_two = call(pack_seed_kernel, kept(t_edge, t_edge), kept(seed, s_one, s_two))
     t_one, t_two = swapped(t_one, t_two, GY)
     grad, back = call(
         functools.partial(adjoint_kernel, grid_x, grid_y),
-        ((block, False), (block, False)),
-        (root, state, later, seed, s_one, s_two, t_one, t_two),
-        scratch=(wide, wide, wide, flat, flat, flat),
+        kept(block, block, space=None),
+        kept(root, state, later, seed, s_one, s_two, t_one, t_two),
+        scratch=[f32(wide)] * 3 + [f32(flat)] * 3,
         flops=20_000_000,
-        limit=12,
-        name="adjoint",
+        limit=6,
     )
 
     near = jnp.sum(from_everyone(partial, ("gx_1", GY)), axis=0)
-    total = jnp.sum(from_everyone(near, FAR))
-    misfit = (0.5 * total / (grid_x * grid_y * depth)).reshape(1)
+    everyone = from_everyone(near, FAR)
+    misfit = (0.5 * jnp.sum(everyone) / (grid_x * grid_y * depth)).reshape(1)
     return (grad, back, final, misfit)
 
 
@@ -555,6 +571,7 @@
         mesh.devices.reshape(ens, along_x // 2, 2, along_y), ("ens", "gx_0", "gx_1", "gy")
     )
     field = P(ENS_GX, "gy", None)
+
     return jax.shard_map(
         on_device,
         mesh=finer,

time: 124 us -> 118 us (0.952)
  local copies, waits for them, and re-layouts: 6.23 us -> 0.64 us
    unnamed x26 -> x8, local copies, waits for them, and re-layouts: 5.61 us -> 0.02 us
    ppermute x4, starting transfers between devices: 24.2 us -> 22.7 us  [swapped(): lax.ppermute(two, axes, back(inner))]
where the time goes in v2:
time: 118 us; the launch traced here: 117 us
  starting transfers between devices  71.1 us (60%)
  waiting for transfers between devices  18.9 us (16%)
  Pallas kernels  14.1 us (12%)
  blocking collectives  8.7 us (7%)
  between operations  3.41 us (3%)
    all_to_all x1, starting transfers between devices, from_everyone(): lax.all_to_all(jnp.broadcast_to(shard[None], (count, *shard.shape)), axis...  45.8 us
    ppermute x4, starting transfers between devices, swapped(): lax.ppermute(two, axes, back(inner))  22.7 us
    all_to_all x1, waiting for transfers between devices, from_everyone(): lax.all_to_all(jnp.broadcast_to(shard[None], (count, *shard.shape)), axis...  16.6 us
    pallas_call x5, Pallas kernels, call(): pl.pallas_call(kernel, out_shape=shapes, in_specs=[pl.BlockSpec(memory_sp...  14.1 us
    all_to_all x1, blocking collectives, from_everyone(): lax.all_to_all(jnp.broadcast_to(shard[None], (count, *shard.shape)), axis...  8.7 us
    ppermute x4, starting transfers between devices, swapped(): lax.ppermute(one, axes, back(outer))  2.67 us
  transfers between devices with their start and end apart: 9, of which 3 were waited for; matrix products, arithmetic and copies ran while one was open for 1% of the time, Pallas kernels for 0%

profile of v2, /device:TPU:40, one launch (start us, length us, event | category | flops | bytes accessed | tf_op | source)
XLA Modules:
  0.0 117.4 jit_solution(421179415950951299)
XLA Ops:
  0.6 0.0 copy-start
  0.6 0.0 copy-start.1
  0.7 1.2 %shard_map.129 = (f32[2,2,128,128]{3,2,1,0:T(8,128)S(1)}, f32[2,2,128,128]{3,2,1,0:T(8,128)S(1)}) custom-call(f32[8,128,128]{2,1,0:T(8,128)} %start_ref.5, f32[8,128,128]{2,1,0:T(8,128)} %cond_ref.5), custom_call_target="tpu_custom_call" | custom-call | flops 1000000 | bytes 1000000 | tf_op jit(solution)/shard_map/pallas_call | solution.py:461
  1.9 0.7 collective-permute-start
  2.6 0.0 copy-start.2
  2.6 0.0 copy-start.3
  2.6 6.2 %collective-permute-start.1 = (f32[2,2,128,128]{3,2,1,0:T(8,128)S(1)}, f32[2,2,128,128]{3,2,1,0:T(8,128)S(1)}, u32[]{:S(2)}, u32[]{:S(2)}) collective-permute-start(f32[2,2,128,128]{3,2,1,0:T(8,128)S(1)} %get-tuple-element.21), channel_id=1, source_target_pairs={{0,4},{8,12},{16,20},{24,28},{32,36},{40,44},{48,52},{56,60},{64,6... | collective-permute-start | bytes 786440 | tf_op jit(solution)/shard_map/ppermute | solution.py:481
  8.8 0.0 collective-permute-done.x_one_ref
  8.8 1.1 collective-permute-done.1.x_two_ref
  10.0 0.0 copy-done
  10.0 0.0 copy-done.1
  10.0 0.7 collective-permute-start.2
  10.7 6.5 %collective-permute-start.3 = (f32[2,12,2,128]{3,2,1,0:T(2,128)S(1)}, f32[2,12,2,128]{3,2,1,0:T(2,128)S(1)}, u32[]{:S(2)}, u32[]{:S(2)}) collective-permute-start(f32[2,12,2,128]{3,2,1,0:T(2,128)S(1)} %get-tuple-element.23), channel_id=1, source_target_pairs={{0,1},{2,3},{1,0},{3,2},{4,5},{6,7},{5,4},{7,6},{8,9},{10,11},{9,8... | collective-permute-start | bytes 73736 | tf_op jit(solution)/shard_map/ppermute | solution.py:481
  18.0 0.0 collective-permute-done.2.y_one_ref
  18.0 1.1 collective-permute-done.3.y_two_ref
  19.1 0.0 copy-done.2
  19.1 0.0 copy-done.3
  19.1 7.7 %shard_map.131 = (f32[12,144,128]{2,1,0:T(8,128)S(1)}, f32[12,144,128]{2,1,0:T(8,128)S(1)}, f32[12,144,128]{2,1,0:T(8,128)S(1)}, f32[8,128,128]{2,1,0:T(8,128)},...) custom-call(f32[1]{0:T(128)S(6)} %add.9.first_factor, ...), custom_call_target="tpu_custom_call" | custom-call | flops 20000000 | bytes 1000000 | tf_op jit(solution)/shard_map/pallas_call | solution.py:461
  26.8 0.7 collective-permute-start.4
  27.4 5.6 %collective-permute-start.5 = (f32[2,128,128]{2,1,0:T(8,128)}, f32[2,128,128]{2,1,0:T(8,128)S(1)}, u32[]{:S(2)}, u32[]{:S(2)}) collective-permute-start(f32[2,128,128]{2,1,0:T(8,128)} %get-tuple-element.29), channel_id=1, source_target_pairs={{0,4},{8,12},{16,20},{24,28},{32,36},{40,44},{48,52},{56,60},{64,6... | collective-permute-start | bytes 393224 | tf_op jit(solution)/shard_map/ppermute | solution.py:481
  33.1 8.7 %all_to_all.10 = f32[8,1,128]{2,1,0:T(1,128)S(1)} all-to-all(f32[8,1,128]{2,1,0:T(1,128)S(1)} %broadcast_in_dim.7), channel_id=1, replica_groups=mesh['ens'=2,'gx_0'=32,'gx_1'=2,'gy'=4] {'gx_1','gy'}, dimensions={0} | all-to-all | bytes 8192 | tf_op jit(solution)/shard_map/all_to_all | solution.py:486
  41.8 0.6 broadcast_in_dim.16
  42.4 45.8 %all-to-all-start.1 = ((f32[32,1,128]{2,1,0:T(1,128)}), f32[32,1,128]{2,1,0:T(1,128)S(1)}, u32[]{:S(2)}, u32[]{:S(2)}) async-start(f32[32,1,128]{2,1,0:T(1,128)} %broadcast_in_dim.16), calls=%async_computation.1 | async-start | bytes 32768 | tf_op jit(solution)/shard_map/all_to_all | solution.py:486
  88.2 0.0 collective-permute-done.4.x_one_ref
  88.2 0.0 collective-permute-done.5.x_two_ref
  88.3 0.7 collective-permute-start.6
  88.9 4.3 %collective-permute-start.7 = (f32[12,2,128]{2,1,0:T(2,128)S(1)}, f32[12,2,128]{2,1,0:T(2,128)S(1)}, u32[]{:S(2)}, u32[]{:S(2)}) collective-permute-start(f32[12,2,128]{2,1,0:T(2,128)S(1)} %get-tuple-element.31), channel_id=1, source_target_pairs={{0,1},{2,3},{1,0},{3,2},{4,5},{6,7},{5,4},{7,6},{8,9},{10,11},{9,8... | collective-permute-start | bytes 36872 | tf_op jit(solution)/shard_map/ppermute | solution.py:481
  93.3 16.6 %all-to-all-done.1 = f32[32,1,128]{2,1,0:T(1,128)S(1)} async-done(((f32[32,1,128]{2,1,0:T(1,128)}), f32[32,1,128]{2,1,0:T(1,128)S(1)}, u32[]{:S(2)}, u32[]{:S(2)}) %all-to-all-start.1) | async-done | bytes 16416 | tf_op jit(solution)/shard_map/all_to_all | solution.py:486
  109.9 0.6 reduce_sum.19
  111.2 0.0 collective-permute-done.6.y_one_ref
  111.2 0.0 collective-permute-done.7.y_two_ref
  111.2 5.1 %shard_map.133 = (f32[8,128,128]{2,1,0:T(8,128)}, f32[8,128,128]{2,1,0:T(8,128)}) custom-call(f32[12,144,128]{2,1,0:T(8,128)S(1)} %get-tuple-element.24.root_ref, f32[12,144,128]{2,1,0:T(8,128)S(1)} %get-tuple-element.25.state_ref, f32[12,144,128]{2,1,0:T(8,128)S(1)} %get-tuple-element.26.next_ref, f32[8,128,128]{2,1,0:T(8,128)S(1)} %get-tuple-element.27.seed_ref, ...), custom_call_target="tpu_custom_call" | custom-call | flops 20000000 | bytes 1000000 | tf_op jit(solution)/shard_map/pallas_call | solution.py:461
  (4 shorter events, 0.1 us)
Async XLA Ops:
  0.6 9.3 %copy-start = (f32[8,128,128]{2,1,0:T(8,128)S(1)}, f32[8,128,128]{2,1,0:T(8,128)}, u32[]{:S(2)}) copy-start(f32[8,128,128]{2,1,0:T(8,128)} %start_ref.5) | copy-start | bytes 1572868
  0.6 9.3 %copy-start.1 = (f32[8,128,128]{2,1,0:T(8,128)S(1)}, f32[8,128,128]{2,1,0:T(8,128)}, u32[]{:S(2)}) copy-start(f32[8,128,128]{2,1,0:T(8,128)} %cond_ref.5) | copy-start | bytes 1572868
  1.9 6.9 %collective-permute-start = (f32[2,2,128,128]{3,2,1,0:T(8,128)S(1)}, f32[2,2,128,128]{3,2,1,0:T(8,128)S(1)}, u32[]{:S(2)}, u32[]{:S(2)}) collective-permute-start(f32[2,2,128,128]{3,2,1,0:T(8,128)S(1)} %get-tuple-element.20), channel_id=1, source_target_pairs={{4,8},{12,16},{20,24},{28,32},{36,40},{44,48},{52,56},{60,64},{68,... | collective-permute-start | bytes 786440 | tf_op jit(solution)/shard_map/ppermute | solution.py:481
  2.6 16.5 %copy-start.2 = (f32[8,128,128]{2,1,0:T(8,128)S(1)}, f32[8,128,128]{2,1,0:T(8,128)}, u32[]{:S(2)}) copy-start(f32[8,128,128]{2,1,0:T(8,128)} %survey_ref.1) | copy-start | bytes 1572868
  2.6 16.5 %copy-start.3 = (f32[8,128,128]{2,1,0:T(8,128)S(1)}, f32[8,128,128]{2,1,0:T(8,128)}, u32[]{:S(2)}) copy-start(f32[8,128,128]{2,1,0:T(8,128)} %weight_ref.1) | copy-start | bytes 1572868
  2.6 7.4 %collective-permute-start.1 = (f32[2,2,128,128]{3,2,1,0:T(8,128)S(1)}, f32[2,2,128,128]{3,2,1,0:T(8,128)S(1)}, u32[]{:S(2)}, u32[]{:S(2)}) collective-permute-start(f32[2,2,128,128]{3,2,1,0:T(8,128)S(1)} %get-tuple-element.21), channel_id=1, source_target_pairs={{0,4},{8,12},{16,20},{24,28},{32,36},{40,44},{48,52},{56,60},{64,6... | collective-permute-start | bytes 786440 | tf_op jit(solution)/shard_map/ppermute | solution.py:481
  10.0 8.0 %collective-permute-start.2 = (f32[2,12,2,128]{3,2,1,0:T(2,128)S(1)}, f32[2,12,2,128]{3,2,1,0:T(2,128)S(1)}, u32[]{:S(2)}, u32[]{:S(2)}) collective-permute-start(f32[2,12,2,128]{3,2,1,0:T(2,128)S(1)} %get-tuple-element.22), channel_id=1, source_target_pairs={{1,2},{2,1},{5,6},{6,5},{9,10},{10,9},{13,14},{14,13},{17,18},{18,... | collective-permute-start | bytes 73736 | tf_op jit(solution)/shard_map/ppermute | solution.py:481
  10.7 8.4 %collective-permute-start.3 = (f32[2,12,2,128]{3,2,1,0:T(2,128)S(1)}, f32[2,12,2,128]{3,2,1,0:T(2,128)S(1)}, u32[]{:S(2)}, u32[]{:S(2)}) collective-permute-start(f32[2,12,2,128]{3,2,1,0:T(2,128)S(1)} %get-tuple-element.23), channel_id=1, source_target_pairs={{0,1},{2,3},{1,0},{3,2},{4,5},{6,7},{5,4},{7,6},{8,9},{10,11},{9,8... | collective-permute-start | bytes 73736 | tf_op jit(solution)/shard_map/ppermute | solution.py:481
  26.8 61.4 %collective-permute-start.4 = (f32[2,128,128]{2,1,0:T(8,128)}, f32[2,128,128]{2,1,0:T(8,128)S(1)}, u32[]{:S(2)}, u32[]{:S(2)}) collective-permute-start(f32[2,128,128]{2,1,0:T(8,128)} %get-tuple-element.28), channel_id=1, source_target_pairs={{4,8},{12,16},{20,24},{28,32},{36,40},{44,48},{52,56},{60,64},{68,... | collective-permute-start | bytes 393224 | tf_op jit(solution)/shard_map/ppermute | solution.py:481
  27.4 60.8 %collective-permute-start.5 = (f32[2,128,128]{2,1,0:T(8,128)}, f32[2,128,128]{2,1,0:T(8,128)S(1)}, u32[]{:S(2)}, u32[]{:S(2)}) collective-permute-start(f32[2,128,128]{2,1,0:T(8,128)} %get-tuple-element.29), channel_id=1, source_target_pairs={{0,4},{8,12},{16,20},{24,28},{32,36},{40,44},{48,52},{56,60},{64,6... | collective-permute-start | bytes 393224 | tf_op jit(solution)/shard_map/ppermute | solution.py:481
  42.4 67.5 %all-to-all-start.1 = ((f32[32,1,128]{2,1,0:T(1,128)}), f32[32,1,128]{2,1,0:T(1,128)S(1)}, u32[]{:S(2)}, u32[]{:S(2)}) async-start(f32[32,1,128]{2,1,0:T(1,128)} %broadcast_in_dim.16), calls=%async_computation.1 | async-start | bytes 32768 | tf_op jit(solution)/shard_map/all_to_all | solution.py:486
  88.3 22.9 %collective-permute-start.6 = (f32[12,2,128]{2,1,0:T(2,128)S(1)}, f32[12,2,128]{2,1,0:T(2,128)S(1)}, u32[]{:S(2)}, u32[]{:S(2)}) collective-permute-start(f32[12,2,128]{2,1,0:T(2,128)S(1)} %get-tuple-element.30), channel_id=1, source_target_pairs={{1,2},{2,1},{5,6},{6,5},{9,10},{10,9},{13,14},{14,13},{17,18},{18,... | collective-permute-start | bytes 36872 | tf_op jit(solution)/shard_map/ppermute | solution.py:481
  88.9 22.3 %collective-permute-start.7 = (f32[12,2,128]{2,1,0:T(2,128)S(1)}, f32[12,2,128]{2,1,0:T(2,128)S(1)}, u32[]{:S(2)}, u32[]{:S(2)}) collective-permute-start(f32[12,2,128]{2,1,0:T(2,128)S(1)} %get-tuple-element.31), channel_id=1, source_target_pairs={{0,1},{2,3},{1,0},{3,2},{4,5},{6,7},{5,4},{7,6},{8,9},{10,11},{9,8... | collective-permute-start | bytes 36872 | tf_op jit(solution)/shard_map/ppermute | solution.py:481

commit v3 on v2

--- a/solution.py
+++ b/solution.py
@@ -22,6 +22,8 @@
 
 RIM = 2
 ROW = 8
+LINES = 1024
+PAD = 8
 
 
 def split(value, size):
@@ -60,25 +62,35 @@
     return jnp.where(is_open, jnp.float32(time_step), jnp.float32(0.0))
 
 
-def visit(count, hit, act):
+def visit(count, outside, act):
     group = math.gcd(count, 8)
 
-    def one(base, inner):
-        @pl.when(hit(base + inner))
+    def one(index):
+        @pl.when(outside(index) >= 0)
         def _():
-            act(base + inner)
-
-    def step(index, carry):
-        base = index * group
-        anyone = functools.reduce(operator.or_, [hit(base + k) for k in range(group)])
-
-        @pl.when(anyone)
+            act(index)
+
+    def step(number, carry):
+        base = number * group
+        everyone = functools.reduce(operator.and_, [outside(base + k) for k in range(group)])
+
+        @pl.when(everyone >= 0)
         def _():
-            lax.fori_loop(0, group, lambda k, c: (one(base, k), c)[1], 0)
+            lax.fori_loop(0, group, lambda k, c: (one(base + k), c)[1], 0)
 
         return carry
 
     lax.fori_loop(0, count // group, step, 0)
+
+
+def start_copies(sources, targets, done):
+    copies = [
+        pltpu.make_async_copy(source, target, done.at[k])
+        for k, (source, target) in enumerate(zip(sources, targets))
+    ]
+    for copy in copies:
+        copy.start()
+    return copies
 
 
 def pack_x_kernel(start_ref, cond_ref, one_ref, two_ref, done):
@@ -149,8 +161,9 @@
     base_one = jnp.where(even_x, shift, RIM + size)
     base_two = shift + RIM + size - base_one
 
+
     def copy_own(k, carry):
-        wide_ref[RIM + k, ROW : ROW + rows] = own(k)
+        wide_ref[RIM + k, ROW : ROW + rows] = own.read(k)
         return carry
 
     lax.fori_loop(0, size, copy_own, 0)
@@ -183,12 +196,18 @@
         self.shape = shape
         self.read = read
 
-    def __call__(self, k):
-        return self.read(k)
-
-
-def forward_kernel(
-    grid_x,
+
+def pack_spot(at_x, at_y, at_z, depth):
+    return ((at_x + RIM) * LINES + at_y + ROW) * depth + at_z
+
+
+def unpack_spot(code, depth):
+    line, at_z = split(code, depth)
+    plane, row = split(line, LINES)
+    return plane, row, at_z
+
+
+def lay_kernel(
     grid_y,
     first_factor,
     second_factor,
@@ -197,8 +216,92 @@
     well_cells_ref,
     well_data_ref,
     well_weight_ref,
+    cond_ref,
+    root_ref,
+    source_spot,
+    first_amount,
+    second_amount,
+    well_spot,
+    well_level,
+    well_pull,
+    source_cells,
+    source_rate,
+    well_cells,
+    well_data,
+    well_weight,
+    done,
+):
+    copies = start_copies(
+        (source_cells_ref, source_rate_ref, well_cells_ref, well_data_ref, well_weight_ref),
+        (source_cells, source_rate, well_cells, well_data, well_weight),
+        done,
+    )
+    size, rows, depth = cond_ref.shape
+    place_x, _ = place_in(GX)
+    place_y, _ = place_in(GY)
+    anchor_x = place_x * size
+    anchor_y = place_y * rows
+    sources = source_cells.shape[0]
+    wells = well_cells.shape[0]
+
+    def own(k, carry):
+        root_ref[k] = jnp.exp(0.5 * cond_ref[k])
+        return carry
+
+    lax.fori_loop(0, size, own, 0)
+    for copy in copies:
+        copy.wait()
+
+    def spot(cell):
+        line, at_z = split(cell, depth)
+        at_x, at_y = split(line, grid_y)
+        return at_x - anchor_x, at_y - anchor_y, at_z
+
+    def outside(cell, rim):
+        at_x, at_y, _ = spot(cell)
+        return (
+            (at_x + rim) | (size - 1 + rim - at_x) | (at_y + rim) | (rows - 1 + rim - at_y)
+        )
+
+    source_spot[sources] = 0
+    well_spot[wells] = 0
+
+    def add_source(index):
+        slot = source_spot[sources]
+        source_spot[slot] = pack_spot(*spot(source_cells[index]), depth)
+        first_amount[slot] = time_step * (source_rate[index] * first_factor[0])
+        second_amount[slot] = time_step * (source_rate[index] * second_factor[0])
+        source_spot[sources] = slot + 1
+
+    visit(sources, lambda i: outside(source_cells[i], RIM - 1), add_source)
+
+    def add_well(index):
+        slot = well_spot[wells]
+        well_spot[slot] = pack_spot(*spot(well_cells[index]), depth)
+        well_level[slot] = well_data[index]
+        well_pull[slot] = well_weight[index]
+        well_spot[wells] = slot + 1
+
+    visit(wells, lambda i: outside(well_cells[i], 0), add_well)
+
+
+def sum_kernel(shares_ref, out_ref):
+    total = jnp.sum(shares_ref[...], axis=0)
+    for k in range(out_ref.shape[0]):
+        out_ref[k] = total
+
+
+def forward_kernel(
+    grid_x,
+    grid_y,
+    source_spot_ref,
+    first_amount_ref,
+    second_amount_ref,
+    well_spot_ref,
+    well_level_ref,
+    well_pull_ref,
+    own_root_ref,
     start_ref,
-    cond_ref,
     x_one_ref,
     x_two_ref,
     y_one_ref,
@@ -215,27 +318,27 @@
     partial_ref,
     row_ref,
     flux_ref,
-    source_cells,
-    source_rate,
-    well_cells,
-    well_data,
-    well_weight,
+    source_spot,
+    first_amount,
+    second_amount,
+    well_spot,
+    well_level,
+    well_pull,
     done,
 ):
-    lists = (
-        (source_cells_ref, source_cells),
-        (source_rate_ref, source_rate),
-        (well_cells_ref, well_cells),
-        (well_data_ref, well_data),
-        (well_weight_ref, well_weight),
-    )
-    copies = [
-        pltpu.make_async_copy(source, target, done.at[k])
-        for k, (source, target) in enumerate(lists)
-    ]
-    for copy in copies:
-        copy.start()
-    size, rows, depth = start_ref.shape
+    copies = start_copies(
+        (
+            source_spot_ref,
+            first_amount_ref,
+            second_amount_ref,
+            well_spot_ref,
+            well_level_ref,
+            well_pull_ref,
+        ),
+        (source_spot, first_amount, second_amount, well_spot, well_level, well_pull),
+        done,
+    )
+    size, rows, depth = survey_ref.shape
     wide = (root_ref.shape[1], depth)
     place_x, even_x = place_in(GX)
     place_y, _ = place_in(GY)
@@ -254,7 +357,7 @@
     spread(
         root_ref,
         RIM,
-        Own((size, rows), lambda k: jnp.exp(0.5 * cond_ref[k])),
+        Own((size, rows), lambda k: own_root_ref[k]),
         lambda k: jnp.exp(0.5 * x_one_ref[1, k]),
         lambda k: jnp.exp(0.5 * x_two_ref[1, k]),
         lambda k: jnp.exp(0.5 * y_one_ref[1, k]),
@@ -282,15 +385,6 @@
         flux_ref[...] = flux_x
         return here - change
 
-    def spot(cell):
-        line, along_z = split(cell, depth)
-        along_x_, along_y = split(line, grid_y)
-        return along_x_ - anchor_x, along_y - anchor_y, along_z
-
-    def within(cell, rim):
-        at_x, at_y, _ = spot(cell)
-        return (at_x >= -rim) & (at_x < size + rim) & (at_y >= -rim) & (at_y < rows + rim)
-
     lane = lax.broadcasted_iota(jnp.int32, (1, depth), 1)
 
     flux_ref[...] = along_x(state_ref, 0)
@@ -304,13 +398,15 @@
     for copy in copies:
         copy.wait()
 
-    def add_first(index):
-        at_x, at_y, at_z = spot(source_cells[index])
-        where = (at_x + RIM, pl.ds(at_y + ROW, 1), slice(None))
-        amount = time_step * (source_rate[index] * first_factor[0])
-        next_ref[where] = next_ref[where] + jnp.where(lane == at_z, amount, 0.0)
-
-    visit(source_cells.shape[0], lambda i: within(source_cells[i], RIM - 1), add_first)
+    sources = source_spot[source_spot.shape[0] - PAD]
+
+    def add_first(index, carry):
+        plane, row, at_z = unpack_spot(source_spot[index], depth)
+        where = (plane, pl.ds(row, 1), slice(None))
+        next_ref[where] = next_ref[where] + jnp.where(lane == at_z, first_amount[index], 0.0)
+        return carry
+
+    lax.fori_loop(0, sources, add_first, 0)
 
     flux_ref[...] = along_x(next_ref, RIM - 1)
 
@@ -320,15 +416,20 @@
 
     lax.fori_loop(0, size, second_step, 0)
 
-    def add_second(index):
-        at_x, at_y, at_z = spot(source_cells[index])
-        where = (at_x, pl.ds(at_y, 1), slice(None))
-        amount = time_step * (source_rate[index] * second_factor[0])
-        final_ref[where] = final_ref[where] + jnp.where(lane == at_z, amount, 0.0)
-
-    visit(source_cells.shape[0], lambda i: within(source_cells[i], 0), add_second)
-
-    partial_ref[...] = jnp.zeros((1, depth), jnp.float32)
+    def add_second(index, carry):
+        plane, row, at_z = unpack_spot(source_spot[index], depth)
+        plane = plane - RIM
+        row = row - ROW
+
+        @pl.when((plane >= 0) & (plane < size) & (row >= 0) & (row < rows))
+        def _():
+            where = (plane, pl.ds(row, 1), slice(None))
+            amount = second_amount[index]
+            final_ref[where] = final_ref[where] + jnp.where(lane == at_z, amount, 0.0)
+
+        return carry
+
+    lax.fori_loop(0, sources, add_second, 0)
 
     def compare(k, total):
         missed = final_ref[k] - survey_ref[k]
@@ -337,17 +438,20 @@
         return total + jnp.sum((seed * missed).reshape(rows // 8, 8, depth), axis=0)
 
     total = lax.fori_loop(0, size, compare, jnp.zeros((8, depth), jnp.float32))
-    partial_ref[...] = jnp.sum(total, axis=0, keepdims=True)
-
-    def observe(index):
-        at_x, at_y, at_z = spot(well_cells[index])
-        where = (at_x, pl.ds(at_y, 1), slice(None))
-        nearby = final_ref[where] - well_data[index]
-        pull = jnp.where(lane == at_z, well_weight[index] * nearby, 0.0)
+
+    def observe(index, total):
+        plane, row, at_z = unpack_spot(well_spot[index], depth)
+        where = (plane - RIM, pl.ds(row - ROW, 1), slice(None))
+        nearby = final_ref[where] - well_level[index]
+        pull = jnp.where(lane == at_z, well_pull[index] * nearby, 0.0)
         seed_ref[where] = seed_ref[where] + pull
-        partial_ref[...] = partial_ref[...] + pull * nearby
-
-    visit(well_cells.shape[0], lambda i: within(well_cells[i], 0), observe)
+        return total + pull * nearby
+
+    wells = well_spot[well_spot.shape[0] - PAD]
+    total = lax.fori_loop(0, wells, observe, jnp.sum(total, axis=0, keepdims=True))
+    total = total * (0.5 / (grid_x * grid_y * depth))
+    for k in range(partial_ref.shape[0]):
+        partial_ref[k] = total
 
     first = jnp.where(even_x, 0, size - RIM)
     second = size - RIM - first
@@ -451,18 +555,23 @@
 
 def call(kernel, outs, operands, *, scratch=(), flops=1_000_000, limit=2):
     shapes = tuple(
-        jax.ShapeDtypeStruct(shape, jnp.float32) if space is None else space(shape, jnp.float32)
+        space(shape, jnp.float32)
+        if space == pltpu.VMEM
+        else jax.ShapeDtypeStruct(*shape)
+        if space == pltpu.SMEM
+        else jax.ShapeDtypeStruct(shape, jnp.float32)
         for shape, space in outs
     )
     arrays = [
         array if space == pltpu.SMEM else pltpu.with_memory_space_constraint(array, space)
         for array, space in operands
     ]
+    out_spaces = [pltpu.VMEM if space is None else space for _, space in outs]
     return pl.pallas_call(
         kernel,
         out_shape=shapes,
         in_specs=[pl.BlockSpec(memory_space=space) for _, space in operands],
-        out_specs=tuple(pl.BlockSpec(memory_space=pltpu.VMEM) for _ in outs),
+        out_specs=tuple(pl.BlockSpec(memory_space=space) for space in out_spaces),
         scratch_shapes=scratch,
         cost_estimate=pl.CostEstimate(flops=flops, transcendentals=0, bytes_accessed=1_000_000),
         compiler_params=pltpu.CompilerParams(vmem_limit_bytes=limit << 20),
@@ -478,14 +587,9 @@
     outer = [(i, i + 1) for i in range(1, count - 1, 2)]
     inner = [(i, i + 1) for i in range(0, count - 1, 2)]
     back = lambda pairs: pairs + [(b, a) for a, b in pairs]
-    return lax.ppermute(one, axes, back(outer)), lax.ppermute(two, axes, back(inner))
-
-
-def from_everyone(shard, axis):
-    count = lax.axis_size(axis)
-    return lax.all_to_all(
-        jnp.broadcast_to(shard[None], (count, *shard.shape)), axis, 0, 0, tiled=True
-    )
+    one = lax.ppermute(one, axes, back(outer))
+    two = lax.ppermute(two, axes, back(inner))
+    return one, two
 
 
 def on_device(
@@ -522,6 +626,29 @@
         scratch=[dma((4,))],
     )
     x_one, x_two = swapped(x_one, x_two, GX)
+
+    lists = (source_cells, source_rate, well_cells, well_data, well_weight)
+    sources = source_cells.shape[0] + PAD
+    wells = well_cells.shape[0] + PAD
+    found = (
+        ((sources,), jnp.int32),
+        ((sources,), jnp.float32),
+        ((sources,), jnp.float32),
+        ((wells,), jnp.int32),
+        ((wells,), jnp.float32),
+        ((wells,), jnp.float32),
+    )
+    root, *hits = call(
+        functools.partial(lay_kernel, grid_y),
+        kept(block) + kept(*found, space=pltpu.SMEM),
+        kept(first_factor, second_factor, space=pltpu.SMEM)
+        + kept(*lists, space=pltpu.HBM)
+        + kept(log_cond),
+        scratch=[pltpu.SMEM(array.shape, array.dtype) for array in lists]
+        + [dma((len(lists),))],
+        flops=4_000_000,
+    )
+
     y_edge = (2, planes, RIM, depth)
     y_one, y_two = call(
         pack_y_kernel, kept(y_edge, y_edge), kept(checkpoint, log_cond, x_one, x_two)
@@ -529,22 +656,26 @@
     y_one, y_two = swapped(y_one, y_two, GY)
 
     s_edge = (RIM, rows, depth)
-    lists = (source_cells, source_rate, well_cells, well_data, well_weight)
-    fields = (checkpoint, log_cond, x_one, x_two, y_one, y_two, survey, survey_weight)
+    near_axes = ("gx_1", GY)
+    near_count = lax.axis_size(near_axes)
+    fields = (root, checkpoint, x_one, x_two, y_one, y_two, survey, survey_weight)
     root, state, later, final, seed, s_one, s_two, partial = call(
         functools.partial(forward_kernel, grid_x, grid_y),
         kept(wide, wide, wide)
         + kept(block, space=None)
-        + kept(block, s_edge, s_edge, (1, depth)),
-        kept(first_factor, second_factor, space=pltpu.SMEM)
-        + kept(*lists, space=pltpu.HBM)
-        + kept(*fields),
+        + kept(block, s_edge, s_edge, (near_count, 1, depth)),
+        kept(*hits, space=pltpu.HBM) + kept(*fields),
         scratch=[f32(flat), f32(flat)]
-        + [pltpu.SMEM(array.shape, array.dtype) for array in lists]
-        + [dma((len(lists),))],
+        + [pltpu.SMEM(array.shape, array.dtype) for array in hits]
+        + [dma((len(hits),))],
         flops=20_000_000,
         limit=4,
     )
+
+    near = lax.all_to_all(partial, near_axes, 0, 0, tiled=True)
+    (near,) = call(sum_kernel, kept((lax.axis_size(FAR), 1, depth)), kept(near))
+    everyone = lax.all_to_all(near, FAR, 0, 0, tiled=True)
+    misfit = jnp.sum(everyone).reshape(1)
 
     s_one, s_two = swapped(s_one, s_two, GX)
     t_edge = (planes, RIM, depth)
@@ -558,10 +689,6 @@
         flops=20_000_000,
         limit=6,
     )
-
-    near = jnp.sum(from_everyone(partial, ("gx_1", GY)), axis=0)
-    everyone = from_everyone(near, FAR)
-    misfit = (0.5 * jnp.sum(everyone) / (grid_x * grid_y * depth)).reshape(1)
     return (grad, back, final, misfit)
 
 

time: 118 us -> 117 us (level)
  local copies, waits for them, and re-layouts: 0.64 us -> 2.77 us
  between operations: 3.41 us -> 1.62 us
  waiting for transfers between devices: 18.9 us -> 17.6 us
  Pallas kernels: 14.1 us -> 15.3 us
    unnamed x8 -> x20, local copies, waits for them, and re-layouts: 0.02 us -> 2.77 us
    pallas_call x5 -> x7, Pallas kernels: 14.1 us -> 15.3 us  [call(): pl.pallas_call(kernel, out_shape=shapes, in_specs=[pl.BlockSpec(memory_sp...]
  transfers between devices with their start and end apart: 9 -> 9, of which waited for: 3 -> 2; matrix products, arithmetic and copies ran while one was open for 1% -> 1% of each run, Pallas kernels for 0% -> 4%
where the time goes in v3:
time: 117 us
  starting transfers between devices  71.1 us (61%)
  waiting for transfers between devices  17.6 us (15%)
  Pallas kernels  15.3 us (13%)
  blocking collectives  7.66 us (7%)
  local copies, waits for them, and re-layouts  2.77 us (2%)
  between operations  1.62 us (1%)
    all_to_all x1, starting transfers between devices, on_device(): everyone = lax.all_to_all(near, FAR, 0, 0, tiled=True)  45.6 us
    ppermute x4, starting transfers between devices, swapped(): two = lax.ppermute(two, axes, back(inner))  22.6 us
    all_to_all x1, waiting for transfers between devices, on_device(): everyone = lax.all_to_all(near, FAR, 0, 0, tiled=True)  16.5 us
    pallas_call x7, Pallas kernels, call(): pl.pallas_call(kernel, out_shape=shapes, in_specs=[pl.BlockSpec(memory_sp...  15.3 us
    all_to_all x1, blocking collectives, on_device(): near = lax.all_to_all(partial, near_axes, 0, 0, tiled=True)  7.66 us
    ppermute x4, starting transfers between devices, swapped(): one = lax.ppermute(one, axes, back(outer))  2.8 us
    unnamed x20, local copies, waits for them, and re-layouts  2.77 us
  transfers between devices with their start and end apart: 9, of which 2 were waited for; matrix products, arithmetic and copies ran while one was open for 1% of the time, Pallas kernels for 4%

profile of v3, /device:TPU:40, one launch (start us, length us, event | category | flops | bytes accessed | tf_op | source)
XLA Modules:
  0.0 116.7 jit_solution(18405909829650460361)
XLA Ops:
  0.6 0.0 copy-start.1
  0.6 0.0 copy-start
  0.7 1.2 %shard_map.130 = (f32[2,2,128,128]{3,2,1,0:T(8,128)S(1)}, f32[2,2,128,128]{3,2,1,0:T(8,128)S(1)}) custom-call(f32[8,128,128]{2,1,0:T(8,128)} %start_ref.5, f32[8,128,128]{2,1,0:T(8,128)} %cond_ref.5), custom_call_target="tpu_custom_call" | custom-call | flops 1000000 | bytes 1000000 | tf_op jit(solution)/shard_map/pallas_call | solution.py:570
  1.9 0.7 collective-permute-start
  2.6 6.1 %collective-permute-start.1 = (f32[2,2,128,128]{3,2,1,0:T(8,128)S(1)}, f32[2,2,128,128]{3,2,1,0:T(8,128)S(1)}, u32[]{:S(2)}, u32[]{:S(2)}) collective-permute-start(f32[2,2,128,128]{3,2,1,0:T(8,128)S(1)} %get-tuple-element.35), channel_id=1, source_target_pairs={{0,4},{8,12},{16,20},{24,28},{32,36},{40,44},{48,52},{56,60},{64,6... | collective-permute-start | bytes 786440 | tf_op jit(solution)/shard_map/ppermute | solution.py:591
  8.7 0.0 collective-permute-done.x_one_ref
  8.7 1.1 collective-permute-done.1.x_two_ref
  9.8 0.0 copy-done.1
  9.8 0.0 copy-done
  9.8 0.0 copy-start.3
  9.8 0.0 copy-start.2
  9.9 0.8 collective-permute-start.2
  10.7 6.5 %collective-permute-start.3 = (f32[2,12,2,128]{3,2,1,0:T(2,128)S(1)}, f32[2,12,2,128]{3,2,1,0:T(2,128)S(1)}, u32[]{:S(2)}, u32[]{:S(2)}) collective-permute-start(f32[2,12,2,128]{3,2,1,0:T(2,128)S(1)} %get-tuple-element.37), channel_id=1, source_target_pairs={{0,1},{2,3},{1,0},{3,2},{4,5},{6,7},{5,4},{7,6},{8,9},{10,11},{9,8... | collective-permute-start | bytes 73736 | tf_op jit(solution)/shard_map/ppermute | solution.py:591
  17.9 3.6 %shard_map.129 = (f32[8,128,128]{2,1,0:T(8,128)S(1)}, s32[72]{0:T(128)S(1)}, f32[72]{0:T(128)S(1)}, f32[72]{0:T(128)S(1)}, s32[264]{0:T(512)S(1)}, /*index=5*/f32[264]{0:T(512)S(1)}, f32[264]{0:T(512)S(1)}) custom-call(f32[1]{0:T(128)S(6)} %add.9.first_factor, f32[1]{0:T(128)S(6)} %add.11.second_factor, s32[64]{0:T(128)} %source_cells_ref.1, ...), custom_call_target="tpu_custom_call" | custom-call | flops 4000000 | bytes 1000000 | tf_op jit(solution)/shard_map/pallas_call | solution.py:570
  21.6 0.0 copy-start.6
  21.6 0.6 copy-done.6
  22.2 0.0 copy-start.7
  22.2 0.5 copy-done.7
  22.7 0.0 copy-start.8
  22.7 0.5 copy-done.8
  23.2 0.0 copy-start.9
  23.2 0.6 copy-done.9
  23.8 0.0 copy-start.4
  23.8 0.0 copy-start.5
  23.8 0.0 collective-permute-done.2.y_one_ref
  23.8 0.0 collective-permute-done.3.y_two_ref
  23.8 0.6 copy-done.4
  24.4 0.0 copy-done.5
  24.4 0.0 copy-done.3
  24.4 0.0 copy-done.2
  24.4 4.7 %shard_map.132 = (f32[12,144,128]{2,1,0:T(8,128)S(1)}, f32[12,144,128]{2,1,0:T(8,128)S(1)}, f32[12,144,128]{2,1,0:T(8,128)S(1)}, f32[8,128,128]{2,1,0:T(8,128)},...) custom-call(s32[72]{0:T(128)} %copy-done.7, ...), custom_call_target="tpu_custom_call" | custom-call | flops 20000000 | bytes 1000000 | tf_op jit(solution)/shard_map/pallas_call | solution.py:570
  29.0 0.7 collective-permute-start.4
  29.7 5.7 %collective-permute-start.5 = (f32[2,128,128]{2,1,0:T(8,128)}, f32[2,128,128]{2,1,0:T(8,128)S(1)}, u32[]{:S(2)}, u32[]{:S(2)}) collective-permute-start(f32[2,128,128]{2,1,0:T(8,128)} %get-tuple-element.43), channel_id=1, source_target_pairs={{0,4},{8,12},{16,20},{24,28},{32,36},{40,44},{48,52},{56,60},{64,6... | collective-permute-start | bytes 393224 | tf_op jit(solution)/shard_map/ppermute | solution.py:591
  35.4 7.7 %all_to_all.10.shares_ref = f32[8,1,128]{2,1,0:T(1,128)S(1)} all-to-all(f32[8,1,128]{2,1,0:T(1,128)S(1)} %get-tuple-element.49), channel_id=1, replica_groups=mesh['ens'=2,'gx_0'=32,'gx_1'=2,'gy'=4] {'gx_1','gy'}, dimensions={0} | all-to-all | bytes 8192 | tf_op jit(solution)/shard_map/all_to_all | solution.py:675
  43.1 0.6 shard_map.135
  43.7 45.6 %all-to-all-start.1 = ((f32[32,1,128]{2,1,0:T(1,128)}), f32[32,1,128]{2,1,0:T(1,128)S(1)}, u32[]{:S(2)}, u32[]{:S(2)}) async-start(f32[32,1,128]{2,1,0:T(1,128)} %shard_map.135), calls=%async_computation.1 | async-start | bytes 32768 | tf_op jit(solution)/shard_map/all_to_all | solution.py:677
  89.4 0.0 collective-permute-done.4.x_one_ref
  89.4 0.0 collective-permute-done.5.x_two_ref
  89.4 0.7 collective-permute-start.6
  90.1 4.4 %collective-permute-start.7 = (f32[12,2,128]{2,1,0:T(2,128)S(1)}, f32[12,2,128]{2,1,0:T(2,128)S(1)}, u32[]{:S(2)}, u32[]{:S(2)}) collective-permute-start(f32[12,2,128]{2,1,0:T(2,128)S(1)} %get-tuple-element.45), channel_id=1, source_target_pairs={{0,1},{2,3},{1,0},{3,2},{4,5},{6,7},{5,4},{7,6},{8,9},{10,11},{9,8... | collective-permute-start | bytes 36872 | tf_op jit(solution)/shard_map/ppermute | solution.py:591
  94.5 16.5 %all-to-all-done.1 = f32[32,1,128]{2,1,0:T(1,128)S(1)} async-done(((f32[32,1,128]{2,1,0:T(1,128)}), f32[32,1,128]{2,1,0:T(1,128)S(1)}, u32[]{:S(2)}, u32[]{:S(2)}) %all-to-all-start.1) | async-done | bytes 16416 | tf_op jit(solution)/shard_map/all_to_all | solution.py:677
  110.9 0.6 reduce_sum.9
  111.6 0.0 collective-permute-done.6.y_one_ref
  111.6 0.0 collective-permute-done.7.y_two_ref
  111.6 5.1 %shard_map.134 = (f32[8,128,128]{2,1,0:T(8,128)}, f32[8,128,128]{2,1,0:T(8,128)}) custom-call(f32[12,144,128]{2,1,0:T(8,128)S(1)} %get-tuple-element.38.root_ref, f32[12,144,128]{2,1,0:T(8,128)S(1)} %get-tuple-element.39.state_ref, f32[12,144,128]{2,1,0:T(8,128)S(1)} %get-tuple-element.40.next_ref, f32[8,128,128]{2,1,0:T(8,128)S(1)} %get-tuple-element.41.seed_ref, ...), custom_call_target="tpu_custom_call" | custom-call | flops 20000000 | bytes 1000000 | tf_op jit(solution)/shard_map/pallas_call | solution.py:570
  (2 shorter events, 0.1 us)
Async XLA Ops:
  0.6 9.2 %copy-start.1 = (f32[8,128,128]{2,1,0:T(8,128)S(1)}, f32[8,128,128]{2,1,0:T(8,128)}, u32[]{:S(2)}) copy-start(f32[8,128,128]{2,1,0:T(8,128)} %start_ref.5) | copy-start | bytes 1572868
  0.6 9.2 %copy-start = (f32[8,128,128]{2,1,0:T(8,128)S(1)}, f32[8,128,128]{2,1,0:T(8,128)}, u32[]{:S(2)}) copy-start(f32[8,128,128]{2,1,0:T(8,128)} %cond_ref.5) | copy-start | bytes 1572868
  1.9 6.8 %collective-permute-start = (f32[2,2,128,128]{3,2,1,0:T(8,128)S(1)}, f32[2,2,128,128]{3,2,1,0:T(8,128)S(1)}, u32[]{:S(2)}, u32[]{:S(2)}) collective-permute-start(f32[2,2,128,128]{3,2,1,0:T(8,128)S(1)} %get-tuple-element.34), channel_id=1, source_target_pairs={{4,8},{12,16},{20,24},{28,32},{36,40},{44,48},{52,56},{60,64},{68,... | collective-permute-start | bytes 786440 | tf_op jit(solution)/shard_map/ppermute | solution.py:590
  2.6 7.2 %collective-permute-start.1 = (f32[2,2,128,128]{3,2,1,0:T(8,128)S(1)}, f32[2,2,128,128]{3,2,1,0:T(8,128)S(1)}, u32[]{:S(2)}, u32[]{:S(2)}) collective-permute-start(f32[2,2,128,128]{3,2,1,0:T(8,128)S(1)} %get-tuple-element.35), channel_id=1, source_target_pairs={{0,4},{8,12},{16,20},{24,28},{32,36},{40,44},{48,52},{56,60},{64,6... | collective-permute-start | bytes 786440 | tf_op jit(solution)/shard_map/ppermute | solution.py:591
  9.8 14.5 %copy-start.3 = (f32[8,128,128]{2,1,0:T(8,128)S(1)}, f32[8,128,128]{2,1,0:T(8,128)}, u32[]{:S(2)}) copy-start(f32[8,128,128]{2,1,0:T(8,128)} %weight_ref.1) | copy-start | bytes 1572868
  9.8 14.5 %copy-start.2 = (f32[8,128,128]{2,1,0:T(8,128)S(1)}, f32[8,128,128]{2,1,0:T(8,128)}, u32[]{:S(2)}) copy-start(f32[8,128,128]{2,1,0:T(8,128)} %survey_ref.1) | copy-start | bytes 1572868
  9.9 13.9 %collective-permute-start.2 = (f32[2,12,2,128]{3,2,1,0:T(2,128)S(1)}, f32[2,12,2,128]{3,2,1,0:T(2,128)S(1)}, u32[]{:S(2)}, u32[]{:S(2)}) collective-permute-start(f32[2,12,2,128]{3,2,1,0:T(2,128)S(1)} %get-tuple-element.36), channel_id=1, source_target_pairs={{1,2},{2,1},{5,6},{6,5},{9,10},{10,9},{13,14},{14,13},{17,18},{18,... | collective-permute-start | bytes 73736 | tf_op jit(solution)/shard_map/ppermute | solution.py:590
  10.7 13.1 %collective-permute-start.3 = (f32[2,12,2,128]{3,2,1,0:T(2,128)S(1)}, f32[2,12,2,128]{3,2,1,0:T(2,128)S(1)}, u32[]{:S(2)}, u32[]{:S(2)}) collective-permute-start(f32[2,12,2,128]{3,2,1,0:T(2,128)S(1)} %get-tuple-element.37), channel_id=1, source_target_pairs={{0,1},{2,3},{1,0},{3,2},{4,5},{6,7},{5,4},{7,6},{8,9},{10,11},{9,8... | collective-permute-start | bytes 73736 | tf_op jit(solution)/shard_map/ppermute | solution.py:591
  21.6 0.6 copy-start.6
  22.2 0.5 copy-start.7
  22.7 0.5 copy-start.8
  23.2 0.6 copy-start.9
  23.8 0.6 copy-start.4
  23.8 0.6 copy-start.5
  29.0 60.3 %collective-permute-start.4 = (f32[2,128,128]{2,1,0:T(8,128)}, f32[2,128,128]{2,1,0:T(8,128)S(1)}, u32[]{:S(2)}, u32[]{:S(2)}) collective-permute-start(f32[2,128,128]{2,1,0:T(8,128)} %get-tuple-element.42), channel_id=1, source_target_pairs={{4,8},{12,16},{20,24},{28,32},{36,40},{44,48},{52,56},{60,64},{68,... | collective-permute-start | bytes 393224 | tf_op jit(solution)/shard_map/ppermute | solution.py:590
  29.7 59.6 %collective-permute-start.5 = (f32[2,128,128]{2,1,0:T(8,128)}, f32[2,128,128]{2,1,0:T(8,128)S(1)}, u32[]{:S(2)}, u32[]{:S(2)}) collective-permute-start(f32[2,128,128]{2,1,0:T(8,128)} %get-tuple-element.43), channel_id=1, source_target_pairs={{0,4},{8,12},{16,20},{24,28},{32,36},{40,44},{48,52},{56,60},{64,6... | collective-permute-start | bytes 393224 | tf_op jit(solution)/shard_map/ppermute | solution.py:591
  43.7 67.2 %all-to-all-start.1 = ((f32[32,1,128]{2,1,0:T(1,128)}), f32[32,1,128]{2,1,0:T(1,128)S(1)}, u32[]{:S(2)}, u32[]{:S(2)}) async-start(f32[32,1,128]{2,1,0:T(1,128)} %shard_map.135), calls=%async_computation.1 | async-start | bytes 32768 | tf_op jit(solution)/shard_map/all_to_all | solution.py:677
  89.4 22.2 %collective-permute-start.6 = (f32[12,2,128]{2,1,0:T(2,128)S(1)}, f32[12,2,128]{2,1,0:T(2,128)S(1)}, u32[]{:S(2)}, u32[]{:S(2)}) collective-permute-start(f32[12,2,128]{2,1,0:T(2,128)S(1)} %get-tuple-element.44), channel_id=1, source_target_pairs={{1,2},{2,1},{5,6},{6,5},{9,10},{10,9},{13,14},{14,13},{17,18},{18,... | collective-permute-start | bytes 36872 | tf_op jit(solution)/shard_map/ppermute | solution.py:590
  90.1 21.5 %collective-permute-start.7 = (f32[12,2,128]{2,1,0:T(2,128)S(1)}, f32[12,2,128]{2,1,0:T(2,128)S(1)}, u32[]{:S(2)}, u32[]{:S(2)}) collective-permute-start(f32[12,2,128]{2,1,0:T(2,128)S(1)} %get-tuple-element.45), channel_id=1, source_target_pairs={{0,1},{2,3},{1,0},{3,2},{4,5},{6,7},{5,4},{7,6},{8,9},{10,11},{9,8... | collective-permute-start | bytes 36872 | tf_op jit(solution)/shard_map/ppermute | solution.py:591

commit v4 on v3

--- a/solution.py
+++ b/solution.py
@@ -62,13 +62,15 @@
     return jnp.where(is_open, jnp.float32(time_step), jnp.float32(0.0))
 
 
-def visit(count, outside, act):
+def visit(count, outside, check, act):
     group = math.gcd(count, 8)
 
     def one(index):
         @pl.when(outside(index) >= 0)
         def _():
-            act(index)
+            @pl.when(check(index))
+            def _():
+                act(index)
 
     def step(number, carry):
         base = number * group
@@ -257,11 +259,15 @@
         at_x, at_y = split(line, grid_y)
         return at_x - anchor_x, at_y - anchor_y, at_z
 
+    layer = grid_y * depth
+
     def outside(cell, rim):
-        at_x, at_y, _ = spot(cell)
-        return (
-            (at_x + rim) | (size - 1 + rim - at_x) | (at_y + rim) | (rows - 1 + rim - at_y)
-        )
+        before = cell - (anchor_x - rim) * layer
+        return before | ((size + 2 * rim) * layer - 1 - before)
+
+    def check(cell, rim):
+        _, at_y, _ = spot(cell)
+        return (at_y >= -rim) & (at_y < rows + rim)
 
     source_spot[sources] = 0
     well_spot[wells] = 0
@@ -273,7 +279,12 @@
         second_amount[slot] = time_step * (source_rate[index] * second_factor[0])
         source_spot[sources] = slot + 1
 
-    visit(sources, lambda i: outside(source_cells[i], RIM - 1), add_source)
+    visit(
+        sources,
+        lambda i: outside(source_cells[i], RIM - 1),
+        lambda i: check(source_cells[i], RIM - 1),
+        add_source,
+    )
 
     def add_well(index):
         slot = well_spot[wells]
@@ -282,7 +293,12 @@
         well_pull[slot] = well_weight[index]
         well_spot[wells] = slot + 1
 
-    visit(wells, lambda i: outside(well_cells[i], 0), add_well)
+    visit(
+        wells,
+        lambda i: outside(well_cells[i], 0),
+        lambda i: check(well_cells[i], 0),
+        add_well,
+    )
 
 
 def sum_kernel(shares_ref, out_ref):
@@ -664,7 +680,7 @@
         kept(wide, wide, wide)
         + kept(block, space=None)
         + kept(block, s_edge, s_edge, (near_count, 1, depth)),
-        kept(*hits, space=pltpu.HBM) + kept(*fields),
+        kept(*hits) + kept(*fields),
         scratch=[f32(flat), f32(flat)]
         + [pltpu.SMEM(array.shape, array.dtype) for array in hits]
         + [dma((len(hits),))],

time: 117 us -> 115 us (0.983)
  local copies, waits for them, and re-layouts: 2.77 us -> 0.02 us
    unnamed x20 -> x8, local copies, waits for them, and re-layouts: 2.77 us -> 0.02 us
    all_to_all x1, starting transfers between devices: 45.6 us -> 47.1 us  [on_device(): everyone = lax.all_to_all(near, FAR, 0, 0, tiled=True)]
where the time goes in v4:
time: 115 us
  starting transfers between devices  71.9 us (63%)
  waiting for transfers between devices  17.8 us (15%)
  Pallas kernels  15.3 us (13%)
  blocking collectives  7.66 us (7%)
  between operations  1.63 us (1%)
    all_to_all x1, starting transfers between devices, on_device(): everyone = lax.all_to_all(near, FAR, 0, 0, tiled=True)  47.1 us
    ppermute x4, starting transfers between devices, swapped(): two = lax.ppermute(two, axes, back(inner))  22 us
    all_to_all x1, waiting for transfers between devices, on_device(): everyone = lax.all_to_all(near, FAR, 0, 0, tiled=True)  16.6 us
    pallas_call x7, Pallas kernels, call(): pl.pallas_call(kernel, out_shape=shapes, in_specs=[pl.BlockSpec(memory_sp...  15.3 us
    all_to_all x1, blocking collectives, on_device(): near = lax.all_to_all(partial, near_axes, 0, 0, tiled=True)  7.66 us
    ppermute x4, starting transfers between devices, swapped(): one = lax.ppermute(one, axes, back(outer))  2.8 us
  transfers between devices with their start and end apart: 9, of which 2 were waited for; matrix products, arithmetic and copies ran while one was open for 1% of the time, Pallas kernels for 4%

profile of v4, /device:TPU:40, one launch (start us, length us, event | category | flops | bytes accessed | tf_op | source)
XLA Modules:
  0.0 114.9 jit_solution(15019560307682538023)
XLA Ops:
  0.6 0.0 copy-start.1
  0.6 0.0 copy-start
  0.7 1.2 %shard_map.130 = (f32[2,2,128,128]{3,2,1,0:T(8,128)S(1)}, f32[2,2,128,128]{3,2,1,0:T(8,128)S(1)}) custom-call(f32[8,128,128]{2,1,0:T(8,128)} %start_ref.5, f32[8,128,128]{2,1,0:T(8,128)} %cond_ref.5), custom_call_target="tpu_custom_call" | custom-call | flops 1000000 | bytes 1000000 | tf_op jit(solution)/shard_map/pallas_call | solution.py:586
  1.9 0.7 collective-permute-start
  2.6 6.1 %collective-permute-start.1 = (f32[2,2,128,128]{3,2,1,0:T(8,128)S(1)}, f32[2,2,128,128]{3,2,1,0:T(8,128)S(1)}, u32[]{:S(2)}, u32[]{:S(2)}) collective-permute-start(f32[2,2,128,128]{3,2,1,0:T(8,128)S(1)} %get-tuple-element.35), channel_id=1, source_target_pairs={{0,4},{8,12},{16,20},{24,28},{32,36},{40,44},{48,52},{56,60},{64,6... | collective-permute-start | bytes 786440 | tf_op jit(solution)/shard_map/ppermute | solution.py:607
  8.7 0.0 collective-permute-done.x_one_ref
  8.7 1.1 collective-permute-done.1.x_two_ref
  9.8 0.0 copy-done.1
  9.8 0.0 copy-done
  9.8 0.0 copy-start.3
  9.8 0.0 copy-start.2
  9.9 0.8 collective-permute-start.2
  10.7 6.5 %collective-permute-start.3 = (f32[2,12,2,128]{3,2,1,0:T(2,128)S(1)}, f32[2,12,2,128]{3,2,1,0:T(2,128)S(1)}, u32[]{:S(2)}, u32[]{:S(2)}) collective-permute-start(f32[2,12,2,128]{3,2,1,0:T(2,128)S(1)} %get-tuple-element.37), channel_id=1, source_target_pairs={{0,1},{2,3},{1,0},{3,2},{4,5},{6,7},{5,4},{7,6},{8,9},{10,11},{9,8... | collective-permute-start | bytes 73736 | tf_op jit(solution)/shard_map/ppermute | solution.py:607
  17.9 3.7 %shard_map.129 = (f32[8,128,128]{2,1,0:T(8,128)S(1)}, s32[72]{0:T(128)S(1)}, f32[72]{0:T(128)S(1)}, f32[72]{0:T(128)S(1)}, s32[264]{0:T(512)S(1)}, /*index=5*/f32[264]{0:T(512)S(1)}, f32[264]{0:T(512)S(1)}) custom-call(f32[1]{0:T(128)S(6)} %add.9.first_factor, f32[1]{0:T(128)S(6)} %add.11.second_factor, s32[64]{0:T(128)} %source_cells_ref.1, ...), custom_call_target="tpu_custom_call" | custom-call | flops 4000000 | bytes 1000000 | tf_op jit(solution)/shard_map/pallas_call | solution.py:586
  21.6 0.0 collective-permute-done.2.y_one_ref
  21.6 0.0 collective-permute-done.3.y_two_ref
  21.6 0.0 copy-done.3
  21.7 0.0 copy-done.2
  21.7 4.7 %shard_map.132 = (f32[12,144,128]{2,1,0:T(8,128)S(1)}, f32[12,144,128]{2,1,0:T(8,128)S(1)}, f32[12,144,128]{2,1,0:T(8,128)S(1)}, f32[8,128,128]{2,1,0:T(8,128)},...) custom-call(s32[72]{0:T(128)S(1)} %get-tuple-element.27.source_spot_ref, ...), custom_call_target="tpu_custom_call" | custom-call | flops 20000000 | bytes 1000000 | tf_op jit(solution)/shard_map/pallas_call | solution.py:586
  26.4 0.7 collective-permute-start.4
  27.0 5.0 %collective-permute-start.5 = (f32[2,128,128]{2,1,0:T(8,128)}, f32[2,128,128]{2,1,0:T(8,128)S(1)}, u32[]{:S(2)}, u32[]{:S(2)}) collective-permute-start(f32[2,128,128]{2,1,0:T(8,128)} %get-tuple-element.43), channel_id=1, source_target_pairs={{0,4},{8,12},{16,20},{24,28},{32,36},{40,44},{48,52},{56,60},{64,6... | collective-permute-start | bytes 393224 | tf_op jit(solution)/shard_map/ppermute | solution.py:607
  32.1 7.7 %all_to_all.10.shares_ref = f32[8,1,128]{2,1,0:T(1,128)S(1)} all-to-all(f32[8,1,128]{2,1,0:T(1,128)S(1)} %get-tuple-element.49), channel_id=1, replica_groups=mesh['ens'=2,'gx_0'=32,'gx_1'=2,'gy'=4] {'gx_1','gy'}, dimensions={0} | all-to-all | bytes 8192 | tf_op jit(solution)/shard_map/all_to_all | solution.py:691
  39.7 0.6 shard_map.135
  40.4 47.1 %all-to-all-start.1 = ((f32[32,1,128]{2,1,0:T(1,128)}), f32[32,1,128]{2,1,0:T(1,128)S(1)}, u32[]{:S(2)}, u32[]{:S(2)}) async-start(f32[32,1,128]{2,1,0:T(1,128)} %shard_map.135), calls=%async_computation.1 | async-start | bytes 32768 | tf_op jit(solution)/shard_map/all_to_all | solution.py:693
  87.5 0.0 collective-permute-done.4.x_one_ref
  87.5 0.0 collective-permute-done.5.x_two_ref
  87.5 0.7 collective-permute-start.6
  88.2 4.4 %collective-permute-start.7 = (f32[12,2,128]{2,1,0:T(2,128)S(1)}, f32[12,2,128]{2,1,0:T(2,128)S(1)}, u32[]{:S(2)}, u32[]{:S(2)}) collective-permute-start(f32[12,2,128]{2,1,0:T(2,128)S(1)} %get-tuple-element.45), channel_id=1, source_target_pairs={{0,1},{2,3},{1,0},{3,2},{4,5},{6,7},{5,4},{7,6},{8,9},{10,11},{9,8... | collective-permute-start | bytes 36872 | tf_op jit(solution)/shard_map/ppermute | solution.py:607
  92.6 16.6 %all-to-all-done.1 = f32[32,1,128]{2,1,0:T(1,128)S(1)} async-done(((f32[32,1,128]{2,1,0:T(1,128)}), f32[32,1,128]{2,1,0:T(1,128)S(1)}, u32[]{:S(2)}, u32[]{:S(2)}) %all-to-all-start.1) | async-done | bytes 16416 | tf_op jit(solution)/shard_map/all_to_all | solution.py:693
  109.2 0.6 reduce_sum.9
  109.8 0.0 collective-permute-done.6.y_one_ref
  109.8 0.0 collective-permute-done.7.y_two_ref
  109.8 5.1 %shard_map.134 = (f32[8,128,128]{2,1,0:T(8,128)}, f32[8,128,128]{2,1,0:T(8,128)}) custom-call(f32[12,144,128]{2,1,0:T(8,128)S(1)} %get-tuple-element.38.root_ref, f32[12,144,128]{2,1,0:T(8,128)S(1)} %get-tuple-element.39.state_ref, f32[12,144,128]{2,1,0:T(8,128)S(1)} %get-tuple-element.40.next_ref, f32[8,128,128]{2,1,0:T(8,128)S(1)} %get-tuple-element.41.seed_ref, ...), custom_call_target="tpu_custom_call" | custom-call | flops 20000000 | bytes 1000000 | tf_op jit(solution)/shard_map/pallas_call | solution.py:586
  (2 shorter events, 0.1 us)
Async XLA Ops:
  0.6 9.2 %copy-start.1 = (f32[8,128,128]{2,1,0:T(8,128)S(1)}, f32[8,128,128]{2,1,0:T(8,128)}, u32[]{:S(2)}) copy-start(f32[8,128,128]{2,1,0:T(8,128)} %start_ref.5) | copy-start | bytes 1572868
  0.6 9.2 %copy-start = (f32[8,128,128]{2,1,0:T(8,128)S(1)}, f32[8,128,128]{2,1,0:T(8,128)}, u32[]{:S(2)}) copy-start(f32[8,128,128]{2,1,0:T(8,128)} %cond_ref.5) | copy-start | bytes 1572868
  1.9 6.8 %collective-permute-start = (f32[2,2,128,128]{3,2,1,0:T(8,128)S(1)}, f32[2,2,128,128]{3,2,1,0:T(8,128)S(1)}, u32[]{:S(2)}, u32[]{:S(2)}) collective-permute-start(f32[2,2,128,128]{3,2,1,0:T(8,128)S(1)} %get-tuple-element.34), channel_id=1, source_target_pairs={{4,8},{12,16},{20,24},{28,32},{36,40},{44,48},{52,56},{60,64},{68,... | collective-permute-start | bytes 786440 | tf_op jit(solution)/shard_map/ppermute | solution.py:606
  2.6 7.2 %collective-permute-start.1 = (f32[2,2,128,128]{3,2,1,0:T(8,128)S(1)}, f32[2,2,128,128]{3,2,1,0:T(8,128)S(1)}, u32[]{:S(2)}, u32[]{:S(2)}) collective-permute-start(f32[2,2,128,128]{3,2,1,0:T(8,128)S(1)} %get-tuple-element.35), channel_id=1, source_target_pairs={{0,4},{8,12},{16,20},{24,28},{32,36},{40,44},{48,52},{56,60},{64,6... | collective-permute-start | bytes 786440 | tf_op jit(solution)/shard_map/ppermute | solution.py:607
  9.8 11.8 %copy-start.3 = (f32[8,128,128]{2,1,0:T(8,128)S(1)}, f32[8,128,128]{2,1,0:T(8,128)}, u32[]{:S(2)}) copy-start(f32[8,128,128]{2,1,0:T(8,128)} %weight_ref.1) | copy-start | bytes 1572868
  9.8 11.8 %copy-start.2 = (f32[8,128,128]{2,1,0:T(8,128)S(1)}, f32[8,128,128]{2,1,0:T(8,128)}, u32[]{:S(2)}) copy-start(f32[8,128,128]{2,1,0:T(8,128)} %survey_ref.1) | copy-start | bytes 1572868
  9.9 11.8 %collective-permute-start.2 = (f32[2,12,2,128]{3,2,1,0:T(2,128)S(1)}, f32[2,12,2,128]{3,2,1,0:T(2,128)S(1)}, u32[]{:S(2)}, u32[]{:S(2)}) collective-permute-start(f32[2,12,2,128]{3,2,1,0:T(2,128)S(1)} %get-tuple-element.36), channel_id=1, source_target_pairs={{1,2},{2,1},{5,6},{6,5},{9,10},{10,9},{13,14},{14,13},{17,18},{18,... | collective-permute-start | bytes 73736 | tf_op jit(solution)/shard_map/ppermute | solution.py:606
  10.7 11.0 %collective-permute-start.3 = (f32[2,12,2,128]{3,2,1,0:T(2,128)S(1)}, f32[2,12,2,128]{3,2,1,0:T(2,128)S(1)}, u32[]{:S(2)}, u32[]{:S(2)}) collective-permute-start(f32[2,12,2,128]{3,2,1,0:T(2,128)S(1)} %get-tuple-element.37), channel_id=1, source_target_pairs={{0,1},{2,3},{1,0},{3,2},{4,5},{6,7},{5,4},{7,6},{8,9},{10,11},{9,8... | collective-permute-start | bytes 73736 | tf_op jit(solution)/shard_map/ppermute | solution.py:607
  26.4 61.1 %collective-permute-start.4 = (f32[2,128,128]{2,1,0:T(8,128)}, f32[2,128,128]{2,1,0:T(8,128)S(1)}, u32[]{:S(2)}, u32[]{:S(2)}) collective-permute-start(f32[2,128,128]{2,1,0:T(8,128)} %get-tuple-element.42), channel_id=1, source_target_pairs={{4,8},{12,16},{20,24},{28,32},{36,40},{44,48},{52,56},{60,64},{68,... | collective-permute-start | bytes 393224 | tf_op jit(solution)/shard_map/ppermute | solution.py:606
  27.0 60.4 %collective-permute-start.5 = (f32[2,128,128]{2,1,0:T(8,128)}, f32[2,128,128]{2,1,0:T(8,128)S(1)}, u32[]{:S(2)}, u32[]{:S(2)}) collective-permute-start(f32[2,128,128]{2,1,0:T(8,128)} %get-tuple-element.43), channel_id=1, source_target_pairs={{0,4},{8,12},{16,20},{24,28},{32,36},{40,44},{48,52},{56,60},{64,6... | collective-permute-start | bytes 393224 | tf_op jit(solution)/shard_map/ppermute | solution.py:607
  40.4 68.8 %all-to-all-start.1 = ((f32[32,1,128]{2,1,0:T(1,128)}), f32[32,1,128]{2,1,0:T(1,128)S(1)}, u32[]{:S(2)}, u32[]{:S(2)}) async-start(f32[32,1,128]{2,1,0:T(1,128)} %shard_map.135), calls=%async_computation.1 | async-start | bytes 32768 | tf_op jit(solution)/shard_map/all_to_all | solution.py:693
  87.5 22.3 %collective-permute-start.6 = (f32[12,2,128]{2,1,0:T(2,128)S(1)}, f32[12,2,128]{2,1,0:T(2,128)S(1)}, u32[]{:S(2)}, u32[]{:S(2)}) collective-permute-start(f32[12,2,128]{2,1,0:T(2,128)S(1)} %get-tuple-element.44), channel_id=1, source_target_pairs={{1,2},{2,1},{5,6},{6,5},{9,10},{10,9},{13,14},{14,13},{17,18},{18,... | collective-permute-start | bytes 36872 | tf_op jit(solution)/shard_map/ppermute | solution.py:606
  88.2 21.6 %collective-permute-start.7 = (f32[12,2,128]{2,1,0:T(2,128)S(1)}, f32[12,2,128]{2,1,0:T(2,128)S(1)}, u32[]{:S(2)}, u32[]{:S(2)}) collective-permute-start(f32[12,2,128]{2,1,0:T(2,128)S(1)} %get-tuple-element.45), channel_id=1, source_target_pairs={{0,1},{2,3},{1,0},{3,2},{4,5},{6,7},{5,4},{7,6},{8,9},{10,11},{9,8... | collective-permute-start | bytes 36872 | tf_op jit(solution)/shard_map/ppermute | solution.py:607

commit v5 on v4

--- a/solution.py
+++ b/solution.py
@@ -62,23 +62,25 @@
     return jnp.where(is_open, jnp.float32(time_step), jnp.float32(0.0))
 
 
-def visit(count, outside, check, act):
+def visit(count, far, outside, act):
     group = math.gcd(count, 8)
+
+    def none_of(test, base):
+        return functools.reduce(operator.and_, [test(base + k) for k in range(group)])
 
     def one(index):
         @pl.when(outside(index) >= 0)
         def _():
-            @pl.when(check(index))
-            def _():
-                act(index)
+            act(index)
 
     def step(number, carry):
         base = number * group
-        everyone = functools.reduce(operator.and_, [outside(base + k) for k in range(group)])
-
-        @pl.when(everyone >= 0)
+
+        @pl.when(none_of(far, base) >= 0)
         def _():
-            lax.fori_loop(0, group, lambda k, c: (one(base + k), c)[1], 0)
+            @pl.when(none_of(outside, base) >= 0)
+            def _():
+                lax.fori_loop(0, group, lambda k, c: (one(base + k), c)[1], 0)
 
         return carry
 
@@ -113,25 +115,25 @@
         copy.wait()
 
 
-def pack_y_kernel(start_ref, cond_ref, x_one_ref, x_two_ref, one_ref, two_ref):
+def pack_y_kernel(start_ref, cond_ref, x_one_ref, x_two_ref, out_ref):
     size, rows = start_ref.shape[:2]
-    _, even = place_in(GY)
-
-    def fill(low_ref, high_ref):
-        for out_ref, begin in ((low_ref, 0), (high_ref, rows - RIM)):
-            span = slice(begin, begin + RIM)
-            for which, own_ref in ((0, start_ref), (1, cond_ref)):
-                out_ref[which, 0:RIM] = x_one_ref[which, :, span, :]
-                out_ref[which, RIM : RIM + size] = own_ref[:, span, :]
-                out_ref[which, RIM + size :] = x_two_ref[which, :, span, :]
-
-    @pl.when(even)
+    place = lax.axis_index(GY)
+    out_ref[place] = jnp.zeros(out_ref.shape[1:], jnp.float32)
+
+    def fill(slot, begin):
+        span = slice(begin, begin + RIM)
+        for which, own_ref in ((0, start_ref), (1, cond_ref)):
+            out_ref[slot, which, 0:RIM] = x_one_ref[which, :, span, :]
+            out_ref[slot, which, RIM : RIM + size] = own_ref[:, span, :]
+            out_ref[slot, which, RIM + size :] = x_two_ref[which, :, span, :]
+
+    @pl.when(place > 0)
     def _():
-        fill(one_ref, two_ref)
-
-    @pl.when(jnp.logical_not(even))
+        fill(place - 1, 0)
+
+    @pl.when(place < out_ref.shape[0] - 1)
     def _():
-        fill(two_ref, one_ref)
+        fill(place + 1, rows - RIM)
 
 
 def pack_seed_kernel(seed_ref, x_one_ref, x_two_ref, one_ref, two_ref):
@@ -155,7 +157,7 @@
         fill(two_ref, one_ref)
 
 
-def spread(wide_ref, rim, own, x_one, x_two, y_one, y_two):
+def spread(wide_ref, rim, own, x_one, x_two, y_one, y_two, y_sorted=False):
     size, rows = own.shape
     shift = RIM - rim
     _, even_x = place_in(GX)
@@ -183,6 +185,10 @@
                 plane = base_two + k - rim - size
             wide_ref[plane, ROW - rim : ROW] = low(k)
             wide_ref[plane, ROW + rows : ROW + rows + rim] = high(k)
+
+    if y_sorted:
+        edges(y_one, y_two)
+        return
 
     @pl.when(even_y)
     def _():
@@ -261,13 +267,17 @@
 
     layer = grid_y * depth
 
-    def outside(cell, rim):
+    layer = grid_y * depth
+
+    def far(cell, rim):
         before = cell - (anchor_x - rim) * layer
         return before | ((size + 2 * rim) * layer - 1 - before)
 
-    def check(cell, rim):
-        _, at_y, _ = spot(cell)
-        return (at_y >= -rim) & (at_y < rows + rim)
+    def outside(cell, rim):
+        at_x, at_y, _ = spot(cell)
+        return (
+            (at_x + rim) | (size - 1 + rim - at_x) | (at_y + rim) | (rows - 1 + rim - at_y)
+        )
 
     source_spot[sources] = 0
     well_spot[wells] = 0
@@ -281,8 +291,8 @@
 
     visit(
         sources,
+        lambda i: far(source_cells[i], RIM - 1),
         lambda i: outside(source_cells[i], RIM - 1),
-        lambda i: check(source_cells[i], RIM - 1),
         add_source,
     )
 
@@ -295,8 +305,8 @@
 
     visit(
         wells,
+        lambda i: far(well_cells[i], 0),
         lambda i: outside(well_cells[i], 0),
-        lambda i: check(well_cells[i], 0),
         add_well,
     )
 
@@ -320,8 +330,7 @@
     start_ref,
     x_one_ref,
     x_two_ref,
-    y_one_ref,
-    y_two_ref,
+    y_ref,
     survey_ref,
     weight_ref,
     root_ref,
@@ -357,9 +366,11 @@
     size, rows, depth = survey_ref.shape
     wide = (root_ref.shape[1], depth)
     place_x, even_x = place_in(GX)
-    place_y, _ = place_in(GY)
+    place_y = lax.axis_index(GY)
     anchor_x = place_x * size
     anchor_y = place_y * rows
+    low = jnp.maximum(place_y - 1, 0)
+    high = jnp.minimum(place_y + 1, y_ref.shape[0] - 1)
 
     spread(
         state_ref,
@@ -367,8 +378,9 @@
         Own((size, rows), lambda k: start_ref[k]),
         lambda k: x_one_ref[0, k],
         lambda k: x_two_ref[0, k],
-        lambda k: y_one_ref[0, k],
-        lambda k: y_two_ref[0, k],
+        lambda k: y_ref[low, 0, k],
+        lambda k: y_ref[high, 0, k],
+        y_sorted=True,
     )
     spread(
         root_ref,
@@ -376,8 +388,9 @@
         Own((size, rows), lambda k: own_root_ref[k]),
         lambda k: jnp.exp(0.5 * x_one_ref[1, k]),
         lambda k: jnp.exp(0.5 * x_two_ref[1, k]),
-        lambda k: jnp.exp(0.5 * y_one_ref[1, k]),
-        lambda k: jnp.exp(0.5 * y_two_ref[1, k]),
+        lambda k: jnp.exp(0.5 * y_ref[low, 1, k]),
+        lambda k: jnp.exp(0.5 * y_ref[high, 1, k]),
+        y_sorted=True,
     )
     row_ref[...] = row_mask(wide, anchor_y, grid_y)
     open_z = lane_mask(wide)
@@ -665,16 +678,14 @@
         flops=4_000_000,
     )
 
-    y_edge = (2, planes, RIM, depth)
-    y_one, y_two = call(
-        pack_y_kernel, kept(y_edge, y_edge), kept(checkpoint, log_cond, x_one, x_two)
-    )
-    y_one, y_two = swapped(y_one, y_two, GY)
+    y_slots = (lax.axis_size(GY), 2, planes, RIM, depth)
+    (edges,) = call(pack_y_kernel, kept(y_slots), kept(checkpoint, log_cond, x_one, x_two))
+    edges = lax.all_to_all(edges, GY, 0, 0, tiled=True)
 
     s_edge = (RIM, rows, depth)
     near_axes = ("gx_1", GY)
     near_count = lax.axis_size(near_axes)
-    fields = (root, checkpoint, x_one, x_two, y_one, y_two, survey, survey_weight)
+    fields = (root, checkpoint, x_one, x_two, edges, survey, survey_weight)
     root, state, later, final, seed, s_one, s_two, partial = call(
         functools.partial(forward_kernel, grid_x, grid_y),
         kept(wide, wide, wide)

time: 115 us -> 121 us (1.052)
  local copies, waits for them, and re-layouts: 0.02 us -> 6 us
  starting transfers between devices: 71.9 us -> 69.3 us
    unnamed x8 -> x16, local copies, waits for them, and re-layouts: 0.02 us -> 6 us
    ppermute x4 -> x3, starting transfers between devices: 22 us -> 16.5 us  [swapped(): two = lax.ppermute(two, axes, back(inner))]
    all_to_all x0 -> x1, starting transfers between devices: none -> 4.59 us  [on_device(): edges = lax.all_to_all(edges, GY, 0, 0, tiled=True)]
    all_to_all x0 -> x1, waiting for transfers between devices: none -> 1.25 us  [on_device(): edges = lax.all_to_all(edges, GY, 0, 0, tiled=True)]
    ppermute x4 -> x3, starting transfers between devices: 2.8 us -> 2 us  [swapped(): one = lax.ppermute(one, axes, back(outer))]
  transfers between devices with their start and end apart: 9 -> 8, of which waited for: 2 -> 3; matrix products, arithmetic and copies ran while one was open for 1% -> 1% of each run, Pallas kernels for 4% -> 3%
where the time goes in v5:
time: 121 us; the launch traced here: 120 us
  starting transfers between devices  69.3 us (57%)
  waiting for transfers between devices  19 us (16%)
  Pallas kernels  15.4 us (13%)
  blocking collectives  8.12 us (7%)
  local copies, waits for them, and re-layouts  6 us (5%)
  between operations  1.59 us (1%)
    all_to_all x1, starting transfers between devices, on_device(): everyone = lax.all_to_all(near, FAR, 0, 0, tiled=True)  46.2 us
    all_to_all x1, waiting for transfers between devices, on_device(): everyone = lax.all_to_all(near, FAR, 0, 0, tiled=True)  16.6 us
    ppermute x3, starting transfers between devices, swapped(): two = lax.ppermute(two, axes, back(inner))  16.5 us
    pallas_call x7, Pallas kernels, call(): pl.pallas_call(kernel, out_shape=shapes, in_specs=[pl.BlockSpec(memory_sp...  15.4 us
    all_to_all x1, blocking collectives, on_device(): near = lax.all_to_all(partial, near_axes, 0, 0, tiled=True)  8.12 us
    unnamed x16, local copies, waits for them, and re-layouts  6 us
    all_to_all x1, starting transfers between devices, on_device(): edges = lax.all_to_all(edges, GY, 0, 0, tiled=True)  4.59 us
  transfers between devices with their start and end apart: 8, of which 3 were waited for; matrix products, arithmetic and copies ran while one was open for 1% of the time, Pallas kernels for 3%

profile of v5, /device:TPU:40, one launch (start us, length us, event | category | flops | bytes accessed | tf_op | source)
XLA Modules:
  0.0 120.2 jit_solution(8429952740391185603)
XLA Ops:
  0.6 0.0 copy-start
  0.6 0.0 copy-start.1
  0.7 1.2 %shard_map.130 = (f32[2,2,128,128]{3,2,1,0:T(8,128)S(1)}, f32[2,2,128,128]{3,2,1,0:T(8,128)S(1)}) custom-call(f32[8,128,128]{2,1,0:T(8,128)} %start_ref.5, f32[8,128,128]{2,1,0:T(8,128)} %cond_ref.5), custom_call_target="tpu_custom_call" | custom-call | flops 1000000 | bytes 1000000 | tf_op jit(solution)/shard_map/pallas_call | solution.py:599
  1.9 0.7 collective-permute-start
  2.6 6.1 %collective-permute-start.1 = (f32[2,2,128,128]{3,2,1,0:T(8,128)S(1)}, f32[2,2,128,128]{3,2,1,0:T(8,128)S(1)}, u32[]{:S(2)}, u32[]{:S(2)}) collective-permute-start(f32[2,2,128,128]{3,2,1,0:T(8,128)S(1)} %get-tuple-element.33), channel_id=1, source_target_pairs={{0,4},{8,12},{16,20},{24,28},{32,36},{40,44},{48,52},{56,60},{64,6... | collective-permute-start | bytes 786440 | tf_op jit(solution)/shard_map/ppermute | solution.py:620
  8.7 0.0 collective-permute-done.x_one_ref
  8.7 1.1 collective-permute-done.1.x_two_ref
  9.8 0.0 copy-done
  9.8 0.0 copy-done.1
  9.8 0.7 shard_map.131
  10.5 4.6 %all-to-all-start = ((f32[4,2,12,2,128]{4,3,2,1,0:T(2,128)}), f32[4,2,12,2,128]{4,3,2,1,0:T(2,128)S(1)}, u32[]{:S(2)}, u32[]{:S(2)}) async-start(f32[4,2,12,2,128]{4,3,2,1,0:T(2,128)} %shard_map.131), calls=%async_computation | async-start | bytes 196608 | tf_op jit(solution)/shard_map/all_to_all | solution.py:683
  15.9 3.2 %shard_map.129 = (f32[8,128,128]{2,1,0:T(8,128)S(1)}, s32[72]{0:T(128)S(1)}, f32[72]{0:T(128)S(1)}, f32[72]{0:T(128)S(1)}, s32[264]{0:T(512)S(1)}, /*index=5*/f32[264]{0:T(512)S(1)}, f32[264]{0:T(512)S(1)}) custom-call(f32[1]{0:T(128)S(6)} %add.9.first_factor, f32[1]{0:T(128)S(6)} %add.11.second_factor, s32[64]{0:T(128)} %source_cells_ref.1, ...), custom_call_target="tpu_custom_call" | custom-call | flops 4000000 | bytes 1000000 | tf_op jit(solution)/shard_map/pallas_call | solution.py:599
  19.1 0.0 copy-start.6
  19.1 0.8 copy-done.6
  19.9 1.3 %all-to-all-done.y_ref = f32[4,2,12,2,128]{4,3,2,1,0:T(2,128)S(1)} async-done(((f32[4,2,12,2,128]{4,3,2,1,0:T(2,128)}), f32[4,2,12,2,128]{4,3,2,1,0:T(2,128)S(1)}, u32[]{:S(2)}, u32[]{:S(2)}) %all-to-all-start) | async-done | bytes 98336 | tf_op jit(solution)/shard_map/all_to_all | solution.py:683
  21.1 0.0 copy-start.4
  21.1 1.0 copy-done.4
  22.2 0.0 copy-start.5
  22.2 1.0 copy-done.5
  23.2 0.0 copy-start.7
  23.2 1.0 copy-done.7
  24.2 4.6 %shard_map.132 = (f32[12,144,128]{2,1,0:T(8,128)S(1)}, f32[12,144,128]{2,1,0:T(8,128)S(1)}, f32[12,144,128]{2,1,0:T(8,128)S(1)}, f32[8,128,128]{2,1,0:T(8,128)},...) custom-call(s32[72]{0:T(128)S(1)} %get-tuple-element.25.source_spot_ref, ...), custom_call_target="tpu_custom_call" | custom-call | flops 20000000 | bytes 1000000 | tf_op jit(solution)/shard_map/pallas_call | solution.py:599
  28.9 0.0 copy-start.2
  28.9 0.9 copy-done.2
  29.8 0.7 collective-permute-start.2
  30.5 6.1 %collective-permute-start.3 = (f32[2,128,128]{2,1,0:T(8,128)}, f32[2,128,128]{2,1,0:T(8,128)S(1)}, u32[]{:S(2)}, u32[]{:S(2)}) collective-permute-start(f32[2,128,128]{2,1,0:T(8,128)} %get-tuple-element.39), channel_id=1, source_target_pairs={{0,4},{8,12},{16,20},{24,28},{32,36},{40,44},{48,52},{56,60},{64,6... | collective-permute-start | bytes 393224 | tf_op jit(solution)/shard_map/ppermute | solution.py:620
  36.5 8.1 %all_to_all.15.shares_ref = f32[8,1,128]{2,1,0:T(1,128)S(1)} all-to-all(f32[8,1,128]{2,1,0:T(1,128)S(1)} %get-tuple-element.45), channel_id=1, replica_groups=mesh['ens'=2,'gx_0'=32,'gx_1'=2,'gy'=4] {'gx_1','gy'}, dimensions={0} | all-to-all | bytes 8192 | tf_op jit(solution)/shard_map/all_to_all | solution.py:702
  44.7 0.6 shard_map.135
  45.3 46.2 %all-to-all-start.2 = ((f32[32,1,128]{2,1,0:T(1,128)}), f32[32,1,128]{2,1,0:T(1,128)S(1)}, u32[]{:S(2)}, u32[]{:S(2)}) async-start(f32[32,1,128]{2,1,0:T(1,128)} %shard_map.135), calls=%async_computation.2 | async-start | bytes 32768 | tf_op jit(solution)/shard_map/all_to_all | solution.py:704
  91.5 0.0 collective-permute-done.2.x_one_ref
  91.5 0.0 collective-permute-done.3.x_two_ref
  91.6 0.7 collective-permute-start.4
  92.3 4.3 %collective-permute-start.5 = (f32[12,2,128]{2,1,0:T(2,128)S(1)}, f32[12,2,128]{2,1,0:T(2,128)S(1)}, u32[]{:S(2)}, u32[]{:S(2)}) collective-permute-start(f32[12,2,128]{2,1,0:T(2,128)S(1)} %get-tuple-element.41), channel_id=1, source_target_pairs={{0,1},{2,3},{1,0},{3,2},{4,5},{6,7},{5,4},{7,6},{8,9},{10,11},{9,8... | collective-permute-start | bytes 36872 | tf_op jit(solution)/shard_map/ppermute | solution.py:620
  96.6 16.6 %all-to-all-done.2 = f32[32,1,128]{2,1,0:T(1,128)S(1)} async-done(((f32[32,1,128]{2,1,0:T(1,128)}), f32[32,1,128]{2,1,0:T(1,128)S(1)}, u32[]{:S(2)}, u32[]{:S(2)}) %all-to-all-start.2) | async-done | bytes 16416 | tf_op jit(solution)/shard_map/all_to_all | solution.py:704
  113.3 0.6 reduce_sum.9
  113.9 0.0 collective-permute-done.4.y_one_ref
  113.9 0.0 collective-permute-done.5.y_two_ref
  113.9 0.0 copy-start.3
  113.9 1.2 copy-done.3
  115.1 5.1 %shard_map.134 = (f32[8,128,128]{2,1,0:T(8,128)}, f32[8,128,128]{2,1,0:T(8,128)}) custom-call(f32[12,144,128]{2,1,0:T(8,128)S(1)} %get-tuple-element.34.root_ref, f32[12,144,128]{2,1,0:T(8,128)S(1)} %get-tuple-element.35.state_ref, f32[12,144,128]{2,1,0:T(8,128)S(1)} %copy-done.3, f32[8,128,128]{2,1,0:T(8,128)S(1)} %get-tuple-element.37.seed_ref, ...), custom_call_target="tpu_custom_call" | custom-call | flops 20000000 | bytes 1000000 | tf_op jit(solution)/shard_map/pallas_call | solution.py:599
  (1 shorter events, 0.0 us)
Async XLA Ops:
  0.6 9.2 %copy-start = (f32[8,128,128]{2,1,0:T(8,128)S(1)}, f32[8,128,128]{2,1,0:T(8,128)}, u32[]{:S(2)}) copy-start(f32[8,128,128]{2,1,0:T(8,128)} %start_ref.5) | copy-start | bytes 1572868
  0.6 9.2 %copy-start.1 = (f32[8,128,128]{2,1,0:T(8,128)S(1)}, f32[8,128,128]{2,1,0:T(8,128)}, u32[]{:S(2)}) copy-start(f32[8,128,128]{2,1,0:T(8,128)} %cond_ref.5) | copy-start | bytes 1572868
  1.9 6.8 %collective-permute-start = (f32[2,2,128,128]{3,2,1,0:T(8,128)S(1)}, f32[2,2,128,128]{3,2,1,0:T(8,128)S(1)}, u32[]{:S(2)}, u32[]{:S(2)}) collective-permute-start(f32[2,2,128,128]{3,2,1,0:T(8,128)S(1)} %get-tuple-element.32), channel_id=1, source_target_pairs={{4,8},{12,16},{20,24},{28,32},{36,40},{44,48},{52,56},{60,64},{68,... | collective-permute-start | bytes 786440 | tf_op jit(solution)/shard_map/ppermute | solution.py:619
  2.6 7.2 %collective-permute-start.1 = (f32[2,2,128,128]{3,2,1,0:T(8,128)S(1)}, f32[2,2,128,128]{3,2,1,0:T(8,128)S(1)}, u32[]{:S(2)}, u32[]{:S(2)}) collective-permute-start(f32[2,2,128,128]{3,2,1,0:T(8,128)S(1)} %get-tuple-element.33), channel_id=1, source_target_pairs={{0,4},{8,12},{16,20},{24,28},{32,36},{40,44},{48,52},{56,60},{64,6... | collective-permute-start | bytes 786440 | tf_op jit(solution)/shard_map/ppermute | solution.py:620
  10.5 10.6 %all-to-all-start = ((f32[4,2,12,2,128]{4,3,2,1,0:T(2,128)}), f32[4,2,12,2,128]{4,3,2,1,0:T(2,128)S(1)}, u32[]{:S(2)}, u32[]{:S(2)}) async-start(f32[4,2,12,2,128]{4,3,2,1,0:T(2,128)} %shard_map.131), calls=%async_computation | async-start | bytes 196608 | tf_op jit(solution)/shard_map/all_to_all | solution.py:683
  19.1 0.8 copy-start.6
  21.1 1.0 copy-start.4
  22.2 1.0 copy-start.5
  23.2 1.0 copy-start.7
  28.9 0.9 copy-start.2
  29.8 61.7 %collective-permute-start.2 = (f32[2,128,128]{2,1,0:T(8,128)}, f32[2,128,128]{2,1,0:T(8,128)S(1)}, u32[]{:S(2)}, u32[]{:S(2)}) collective-permute-start(f32[2,128,128]{2,1,0:T(8,128)} %get-tuple-element.38), channel_id=1, source_target_pairs={{4,8},{12,16},{20,24},{28,32},{36,40},{44,48},{52,56},{60,64},{68,... | collective-permute-start | bytes 393224 | tf_op jit(solution)/shard_map/ppermute | solution.py:619
  30.5 61.1 %collective-permute-start.3 = (f32[2,128,128]{2,1,0:T(8,128)}, f32[2,128,128]{2,1,0:T(8,128)S(1)}, u32[]{:S(2)}, u32[]{:S(2)}) collective-permute-start(f32[2,128,128]{2,1,0:T(8,128)} %get-tuple-element.39), channel_id=1, source_target_pairs={{0,4},{8,12},{16,20},{24,28},{32,36},{40,44},{48,52},{56,60},{64,6... | collective-permute-start | bytes 393224 | tf_op jit(solution)/shard_map/ppermute | solution.py:620
  45.3 68.0 %all-to-all-start.2 = ((f32[32,1,128]{2,1,0:T(1,128)}), f32[32,1,128]{2,1,0:T(1,128)S(1)}, u32[]{:S(2)}, u32[]{:S(2)}) async-start(f32[32,1,128]{2,1,0:T(1,128)} %shard_map.135), calls=%async_computation.2 | async-start | bytes 32768 | tf_op jit(solution)/shard_map/all_to_all | solution.py:704
  91.6 22.3 %collective-permute-start.4 = (f32[12,2,128]{2,1,0:T(2,128)S(1)}, f32[12,2,128]{2,1,0:T(2,128)S(1)}, u32[]{:S(2)}, u32[]{:S(2)}) collective-permute-start(f32[12,2,128]{2,1,0:T(2,128)S(1)} %get-tuple-element.40), channel_id=1, source_target_pairs={{1,2},{2,1},{5,6},{6,5},{9,10},{10,9},{13,14},{14,13},{17,18},{18,... | collective-permute-start | bytes 36872 | tf_op jit(solution)/shard_map/ppermute | solution.py:619
  92.3 21.6 %collective-permute-start.5 = (f32[12,2,128]{2,1,0:T(2,128)S(1)}, f32[12,2,128]{2,1,0:T(2,128)S(1)}, u32[]{:S(2)}, u32[]{:S(2)}) collective-permute-start(f32[12,2,128]{2,1,0:T(2,128)S(1)} %get-tuple-element.41), channel_id=1, source_target_pairs={{0,1},{2,3},{1,0},{3,2},{4,5},{6,7},{5,4},{7,6},{8,9},{10,11},{9,8... | collective-permute-start | bytes 36872 | tf_op jit(solution)/shard_map/ppermute | solution.py:620
  113.9 1.2 copy-start.3

commit v6 on v3

--- a/solution.py
+++ b/solution.py
@@ -62,8 +62,11 @@
     return jnp.where(is_open, jnp.float32(time_step), jnp.float32(0.0))
 
 
-def visit(count, outside, act):
+def visit(count, far, outside, act):
     group = math.gcd(count, 8)
+
+    def none_of(test, base):
+        return functools.reduce(operator.and_, [test(base + k) for k in range(group)])
 
     def one(index):
         @pl.when(outside(index) >= 0)
@@ -72,11 +75,12 @@
 
     def step(number, carry):
         base = number * group
-        everyone = functools.reduce(operator.and_, [outside(base + k) for k in range(group)])
-
-        @pl.when(everyone >= 0)
+
+        @pl.when(none_of(far, base) >= 0)
         def _():
-            lax.fori_loop(0, group, lambda k, c: (one(base + k), c)[1], 0)
+            @pl.when(none_of(outside, base) >= 0)
+            def _():
+                lax.fori_loop(0, group, lambda k, c: (one(base + k), c)[1], 0)
 
         return carry
 
@@ -207,55 +211,19 @@
     return plane, row, at_z
 
 
-def lay_kernel(
-    grid_y,
-    first_factor,
-    second_factor,
-    source_cells_ref,
-    source_rate_ref,
-    well_cells_ref,
-    well_data_ref,
-    well_weight_ref,
-    cond_ref,
-    root_ref,
-    source_spot,
-    first_amount,
-    second_amount,
-    well_spot,
-    well_level,
-    well_pull,
-    source_cells,
-    source_rate,
-    well_cells,
-    well_data,
-    well_weight,
-    done,
-):
-    copies = start_copies(
-        (source_cells_ref, source_rate_ref, well_cells_ref, well_data_ref, well_weight_ref),
-        (source_cells, source_rate, well_cells, well_data, well_weight),
-        done,
-    )
-    size, rows, depth = cond_ref.shape
-    place_x, _ = place_in(GX)
-    place_y, _ = place_in(GY)
-    anchor_x = place_x * size
-    anchor_y = place_y * rows
-    sources = source_cells.shape[0]
-    wells = well_cells.shape[0]
-
-    def own(k, carry):
-        root_ref[k] = jnp.exp(0.5 * cond_ref[k])
-        return carry
-
-    lax.fori_loop(0, size, own, 0)
-    for copy in copies:
-        copy.wait()
+def finder(size, rows, depth, grid_y):
+    anchor_x = lax.axis_index(GX) * size
+    anchor_y = lax.axis_index(GY) * rows
+    layer = grid_y * depth
 
     def spot(cell):
         line, at_z = split(cell, depth)
         at_x, at_y = split(line, grid_y)
         return at_x - anchor_x, at_y - anchor_y, at_z
+
+    def far(cell, rim):
+        before = cell - (anchor_x - rim) * layer
+        return before | ((size + 2 * rim) * layer - 1 - before)
 
     def outside(cell, rim):
         at_x, at_y, _ = spot(cell)
@@ -263,26 +231,85 @@
             (at_x + rim) | (size - 1 + rim - at_x) | (at_y + rim) | (rows - 1 + rim - at_y)
         )
 
-    source_spot[sources] = 0
-    well_spot[wells] = 0
-
-    def add_source(index):
-        slot = source_spot[sources]
-        source_spot[slot] = pack_spot(*spot(source_cells[index]), depth)
-        first_amount[slot] = time_step * (source_rate[index] * first_factor[0])
-        second_amount[slot] = time_step * (source_rate[index] * second_factor[0])
-        source_spot[sources] = slot + 1
-
-    visit(sources, lambda i: outside(source_cells[i], RIM - 1), add_source)
-
-    def add_well(index):
-        slot = well_spot[wells]
-        well_spot[slot] = pack_spot(*spot(well_cells[index]), depth)
-        well_level[slot] = well_data[index]
-        well_pull[slot] = well_weight[index]
-        well_spot[wells] = slot + 1
-
-    visit(wells, lambda i: outside(well_cells[i], 0), add_well)
+    def packed(cell):
+        return pack_spot(*spot(cell), depth)
+
+    return far, outside, packed
+
+
+def lay_kernel(
+    grid_y,
+    first_factor,
+    second_factor,
+    cells_ref,
+    rate_ref,
+    cond_ref,
+    root_ref,
+    spot_ref,
+    first_ref,
+    second_ref,
+    cells,
+    rate,
+    done,
+):
+    copies = start_copies((cells_ref, rate_ref), (cells, rate), done)
+    size, rows, depth = cond_ref.shape
+    count = cells.shape[0]
+
+    def own(k, carry):
+        root_ref[k] = jnp.exp(0.5 * cond_ref[k])
+        return carry
+
+    lax.fori_loop(0, size, own, 0)
+    for copy in copies:
+        copy.wait()
+    far, outside, packed = finder(size, rows, depth, grid_y)
+    spot_ref[count] = 0
+
+    def add(index):
+        slot = spot_ref[count]
+        spot_ref[slot] = packed(cells[index])
+        first_ref[slot] = time_step * (rate[index] * first_factor[0])
+        second_ref[slot] = time_step * (rate[index] * second_factor[0])
+        spot_ref[count] = slot + 1
+
+    visit(
+        count,
+        lambda i: far(cells[i], RIM - 1),
+        lambda i: outside(cells[i], RIM - 1),
+        add,
+    )
+
+
+def find_kernel(
+    block,
+    grid_y,
+    cells_ref,
+    data_ref,
+    weight_ref,
+    spot_ref,
+    level_ref,
+    pull_ref,
+    cells,
+    data,
+    weight,
+    done,
+):
+    copies = start_copies((cells_ref, data_ref, weight_ref), (cells, data, weight), done)
+    count = cells.shape[0]
+    far, outside, packed = finder(*block, grid_y)
+    spot_ref[count] = 0
+    for copy in copies:
+        copy.wait()
+
+    def add(index):
+        slot = spot_ref[count]
+        spot_ref[slot] = packed(cells[index])
+        level_ref[slot] = data[index]
+        pull_ref[slot] = weight[index]
+        spot_ref[count] = slot + 1
+
+    visit(count, lambda i: far(cells[i], 0), lambda i: outside(cells[i], 0), add)
 
 
 def sum_kernel(shares_ref, out_ref):
@@ -627,27 +654,35 @@
     )
     x_one, x_two = swapped(x_one, x_two, GX)
 
-    lists = (source_cells, source_rate, well_cells, well_data, well_weight)
     sources = source_cells.shape[0] + PAD
     wells = well_cells.shape[0] + PAD
-    found = (
-        ((sources,), jnp.int32),
-        ((sources,), jnp.float32),
-        ((sources,), jnp.float32),
-        ((wells,), jnp.int32),
-        ((wells,), jnp.float32),
-        ((wells,), jnp.float32),
-    )
-    root, *hits = call(
+
+    def found(count):
+        spaces = (((count,), jnp.int32), ((count,), jnp.float32), ((count,), jnp.float32))
+        return kept(*spaces, space=pltpu.SMEM)
+
+    def held(arrays):
+        return [pltpu.SMEM(array.shape, array.dtype) for array in arrays] + [dma((len(arrays),))]
+
+    source_lists = (source_cells, source_rate)
+    well_lists = (well_cells, well_data, well_weight)
+    root, *source_hits = call(
         functools.partial(lay_kernel, grid_y),
-        kept(block) + kept(*found, space=pltpu.SMEM),
+        kept(block) + found(sources),
         kept(first_factor, second_factor, space=pltpu.SMEM)
-        + kept(*lists, space=pltpu.HBM)
+        + kept(*source_lists)
         + kept(log_cond),
-        scratch=[pltpu.SMEM(array.shape, array.dtype) for array in lists]
-        + [dma((len(lists),))],
+        scratch=held(source_lists),
         flops=4_000_000,
     )
+    well_hits = call(
+        functools.partial(find_kernel, block, grid_y),
+        found(wells),
+        kept(*well_lists),
+        scratch=held(well_lists),
+        flops=4_000_000,
+    )
+    hits = (*source_hits, *well_hits)
 
     y_edge = (2, planes, RIM, depth)
     y_one, y_two = call(
@@ -664,10 +699,8 @@
         kept(wide, wide, wide)
         + kept(block, space=None)
         + kept(block, s_edge, s_edge, (near_count, 1, depth)),
-        kept(*hits, space=pltpu.HBM) + kept(*fields),
-        scratch=[f32(flat), f32(flat)]
-        + [pltpu.SMEM(array.shape, array.dtype) for array in hits]
-        + [dma((len(hits),))],
+        kept(*hits) + kept(*fields),
+        scratch=[f32(flat), f32(flat)] + held(hits),
         flops=20_000_000,
         limit=4,
     )

time: 117 us -> 115 us (0.983)
  local copies, waits for them, and re-layouts: 2.77 us -> 0.05 us
    unnamed x20 -> x18, local copies, waits for them, and re-layouts: 2.77 us -> 0.05 us
    pallas_call x7 -> x8, Pallas kernels: 15.3 us -> 15.9 us  [call(): pl.pallas_call(kernel, out_shape=shapes, in_specs=[pl.BlockSpec(memory_sp...]
where the time goes in v6:
time: 115 us
  starting transfers between devices  71.1 us (62%)
  waiting for transfers between devices  17.6 us (15%)
  Pallas kernels  15.9 us (14%)
  blocking collectives  7.66 us (7%)
  between operations  1.71 us (1%)
    all_to_all x1, starting transfers between devices, on_device(): everyone = lax.all_to_all(near, FAR, 0, 0, tiled=True)  45.9 us
    ppermute x4, starting transfers between devices, swapped(): two = lax.ppermute(two, axes, back(inner))  22.5 us
    all_to_all x1, waiting for transfers between devices, on_device(): everyone = lax.all_to_all(near, FAR, 0, 0, tiled=True)  16.5 us
    pallas_call x8, Pallas kernels, call(): pl.pallas_call(kernel, out_shape=shapes, in_specs=[pl.BlockSpec(memory_sp...  15.9 us
    all_to_all x1, blocking collectives, on_device(): near = lax.all_to_all(partial, near_axes, 0, 0, tiled=True)  7.66 us
    ppermute x4, starting transfers between devices, swapped(): one = lax.ppermute(one, axes, back(outer))  2.8 us
  transfers between devices with their start and end apart: 9, of which 2 were waited for; matrix products, arithmetic and copies ran while one was open for 1% of the time, Pallas kernels for 4%

profile of v6, /device:TPU:40, one launch (start us, length us, event | category | flops | bytes accessed | tf_op | source)
XLA Modules:
  0.0 114.7 jit_solution(5129155039254743599)
XLA Ops:
  0.6 0.0 copy-start.1
  0.6 0.0 copy-start
  0.7 1.2 %shard_map.131 = (f32[2,2,128,128]{3,2,1,0:T(8,128)S(1)}, f32[2,2,128,128]{3,2,1,0:T(8,128)S(1)}) custom-call(f32[8,128,128]{2,1,0:T(8,128)} %start_ref.5, f32[8,128,128]{2,1,0:T(8,128)} %cond_ref.5), custom_call_target="tpu_custom_call" | custom-call | flops 1000000 | bytes 1000000 | tf_op jit(solution)/shard_map/pallas_call | solution.py:597
  1.9 0.7 collective-permute-start
  2.6 6.1 %collective-permute-start.1 = (f32[2,2,128,128]{3,2,1,0:T(8,128)S(1)}, f32[2,2,128,128]{3,2,1,0:T(8,128)S(1)}, u32[]{:S(2)}, u32[]{:S(2)}) collective-permute-start(f32[2,2,128,128]{3,2,1,0:T(8,128)S(1)} %get-tuple-element.35), channel_id=1, source_target_pairs={{0,4},{8,12},{16,20},{24,28},{32,36},{40,44},{48,52},{56,60},{64,6... | collective-permute-start | bytes 786440 | tf_op jit(solution)/shard_map/ppermute | solution.py:618
  8.7 0.0 collective-permute-done.x_one_ref
  8.7 1.1 collective-permute-done.1.x_two_ref
  9.8 0.0 copy-done.1
  9.8 0.0 copy-done
  9.8 0.0 copy-start.6
  9.8 0.0 copy-start.7
  9.8 0.0 copy-start.8
  9.8 0.0 copy-start.4
  9.8 0.0 copy-start.5
  9.9 0.0 copy-start.3
  9.9 0.0 copy-start.2
  9.9 0.8 collective-permute-start.2
  10.7 6.5 %collective-permute-start.3 = (f32[2,12,2,128]{3,2,1,0:T(2,128)S(1)}, f32[2,12,2,128]{3,2,1,0:T(2,128)S(1)}, u32[]{:S(2)}, u32[]{:S(2)}) collective-permute-start(f32[2,12,2,128]{3,2,1,0:T(2,128)S(1)} %get-tuple-element.37), channel_id=1, source_target_pairs={{0,1},{2,3},{1,0},{3,2},{4,5},{6,7},{5,4},{7,6},{8,9},{10,11},{9,8... | collective-permute-start | bytes 73736 | tf_op jit(solution)/shard_map/ppermute | solution.py:618
  18.0 0.0 copy-done.6
  18.0 0.0 copy-done.7
  18.0 0.0 copy-done.8
  18.0 2.5 %shard_map.130 = (s32[264]{0:T(512)S(1)}, f32[264]{0:T(512)S(1)}, f32[264]{0:T(512)S(1)}) custom-call(s32[256]{0:T(256)S(1)} %copy-done.6, f32[256]{0:T(256)S(1)} %copy-done.7, f32[256]{0:T(256)S(1)} %copy-done.8), custom_call_target="tpu_custom_call" | custom-call | flops 4000000 | bytes 1000000 | tf_op jit(solution)/shard_map/pallas_call | solution.py:597
  20.5 0.0 copy-done.4
  20.5 0.0 copy-done.5
  20.5 1.7 %shard_map.129 = (f32[8,128,128]{2,1,0:T(8,128)S(1)}, s32[72]{0:T(128)S(1)}, f32[72]{0:T(128)S(1)}, f32[72]{0:T(128)S(1)}) custom-call(f32[1]{0:T(128)S(6)} %add.9.first_factor, f32[1]{0:T(128)S(6)} %add.11.second_factor, s32[64]{0:T(128)S(1)} %copy-done.4, f32[64]{0:T(128)S(1)} %copy-done.5, f32[8,128,128]{2,1,0:T(8,128)S(1)} %copy-done), custom_call_target="tpu_custom_call" | custom-call | flops 4000000 | bytes 1000000 | tf_op jit(solution)/shard_map/pallas_call | solution.py:597
  22.2 0.0 collective-permute-done.2.y_one_ref
  22.3 0.0 collective-permute-done.3.y_two_ref
  22.3 0.0 copy-done.3
  22.3 0.0 copy-done.2
  22.3 4.7 %shard_map.133 = (f32[12,144,128]{2,1,0:T(8,128)S(1)}, f32[12,144,128]{2,1,0:T(8,128)S(1)}, f32[12,144,128]{2,1,0:T(8,128)S(1)}, f32[8,128,128]{2,1,0:T(8,128)},...) custom-call(s32[72]{0:T(128)S(1)} %get-tuple-element.27.source_spot_ref, ...), custom_call_target="tpu_custom_call" | custom-call | flops 20000000 | bytes 1000000 | tf_op jit(solution)/shard_map/pallas_call | solution.py:597
  27.0 0.7 collective-permute-start.4
  27.7 5.5 %collective-permute-start.5 = (f32[2,128,128]{2,1,0:T(8,128)}, f32[2,128,128]{2,1,0:T(8,128)S(1)}, u32[]{:S(2)}, u32[]{:S(2)}) collective-permute-start(f32[2,128,128]{2,1,0:T(8,128)} %get-tuple-element.43), channel_id=1, source_target_pairs={{0,4},{8,12},{16,20},{24,28},{32,36},{40,44},{48,52},{56,60},{64,6... | collective-permute-start | bytes 393224 | tf_op jit(solution)/shard_map/ppermute | solution.py:618
  33.2 7.7 %all_to_all.10.shares_ref = f32[8,1,128]{2,1,0:T(1,128)S(1)} all-to-all(f32[8,1,128]{2,1,0:T(1,128)S(1)} %get-tuple-element.49), channel_id=1, replica_groups=mesh['ens'=2,'gx_0'=32,'gx_1'=2,'gy'=4] {'gx_1','gy'}, dimensions={0} | all-to-all | bytes 8192 | tf_op jit(solution)/shard_map/all_to_all | solution.py:708
  40.9 0.6 shard_map.136
  41.5 45.9 %all-to-all-start.1 = ((f32[32,1,128]{2,1,0:T(1,128)}), f32[32,1,128]{2,1,0:T(1,128)S(1)}, u32[]{:S(2)}, u32[]{:S(2)}) async-start(f32[32,1,128]{2,1,0:T(1,128)} %shard_map.136), calls=%async_computation.1 | async-start | bytes 32768 | tf_op jit(solution)/shard_map/all_to_all | solution.py:710
  87.4 0.0 collective-permute-done.4.x_one_ref
  87.4 0.0 collective-permute-done.5.x_two_ref
  87.4 0.7 collective-permute-start.6
  88.1 4.4 %collective-permute-start.7 = (f32[12,2,128]{2,1,0:T(2,128)S(1)}, f32[12,2,128]{2,1,0:T(2,128)S(1)}, u32[]{:S(2)}, u32[]{:S(2)}) collective-permute-start(f32[12,2,128]{2,1,0:T(2,128)S(1)} %get-tuple-element.45), channel_id=1, source_target_pairs={{0,1},{2,3},{1,0},{3,2},{4,5},{6,7},{5,4},{7,6},{8,9},{10,11},{9,8... | collective-permute-start | bytes 36872 | tf_op jit(solution)/shard_map/ppermute | solution.py:618
  92.5 16.5 %all-to-all-done.1 = f32[32,1,128]{2,1,0:T(1,128)S(1)} async-done(((f32[32,1,128]{2,1,0:T(1,128)}), f32[32,1,128]{2,1,0:T(1,128)S(1)}, u32[]{:S(2)}, u32[]{:S(2)}) %all-to-all-start.1) | async-done | bytes 16416 | tf_op jit(solution)/shard_map/all_to_all | solution.py:710
  108.9 0.6 reduce_sum.9
  109.6 0.0 collective-permute-done.6.y_one_ref
  109.6 0.0 collective-permute-done.7.y_two_ref
  109.6 5.1 %shard_map.135 = (f32[8,128,128]{2,1,0:T(8,128)}, f32[8,128,128]{2,1,0:T(8,128)}) custom-call(f32[12,144,128]{2,1,0:T(8,128)S(1)} %get-tuple-element.38.root_ref, f32[12,144,128]{2,1,0:T(8,128)S(1)} %get-tuple-element.39.state_ref, f32[12,144,128]{2,1,0:T(8,128)S(1)} %get-tuple-element.40.next_ref, f32[8,128,128]{2,1,0:T(8,128)S(1)} %get-tuple-element.41.seed_ref, ...), custom_call_target="tpu_custom_call" | custom-call | flops 20000000 | bytes 1000000 | tf_op jit(solution)/shard_map/pallas_call | solution.py:597
  (2 shorter events, 0.1 us)
Async XLA Ops:
  0.6 9.2 %copy-start.1 = (f32[8,128,128]{2,1,0:T(8,128)S(1)}, f32[8,128,128]{2,1,0:T(8,128)}, u32[]{:S(2)}) copy-start(f32[8,128,128]{2,1,0:T(8,128)} %start_ref.5) | copy-start | bytes 1572868
  0.6 9.2 %copy-start = (f32[8,128,128]{2,1,0:T(8,128)S(1)}, f32[8,128,128]{2,1,0:T(8,128)}, u32[]{:S(2)}) copy-start(f32[8,128,128]{2,1,0:T(8,128)} %cond_ref.5) | copy-start | bytes 1572868
  1.9 6.8 %collective-permute-start = (f32[2,2,128,128]{3,2,1,0:T(8,128)S(1)}, f32[2,2,128,128]{3,2,1,0:T(8,128)S(1)}, u32[]{:S(2)}, u32[]{:S(2)}) collective-permute-start(f32[2,2,128,128]{3,2,1,0:T(8,128)S(1)} %get-tuple-element.34), channel_id=1, source_target_pairs={{4,8},{12,16},{20,24},{28,32},{36,40},{44,48},{52,56},{60,64},{68,... | collective-permute-start | bytes 786440 | tf_op jit(solution)/shard_map/ppermute | solution.py:617
  2.6 7.2 %collective-permute-start.1 = (f32[2,2,128,128]{3,2,1,0:T(8,128)S(1)}, f32[2,2,128,128]{3,2,1,0:T(8,128)S(1)}, u32[]{:S(2)}, u32[]{:S(2)}) collective-permute-start(f32[2,2,128,128]{3,2,1,0:T(8,128)S(1)} %get-tuple-element.35), channel_id=1, source_target_pairs={{0,4},{8,12},{16,20},{24,28},{32,36},{40,44},{48,52},{56,60},{64,6... | collective-permute-start | bytes 786440 | tf_op jit(solution)/shard_map/ppermute | solution.py:618
  9.8 8.2 %copy-start.6 = (s32[256]{0:T(256)S(1)}, s32[256]{0:T(256)}, u32[]{:S(2)}) copy-start(s32[256]{0:T(256)} %cells_ref.3) | copy-start | bytes 3076
  9.8 8.2 %copy-start.7 = (f32[256]{0:T(256)S(1)}, f32[256]{0:T(256)}, u32[]{:S(2)}) copy-start(f32[256]{0:T(256)} %data_ref.1) | copy-start | bytes 3076
  9.8 8.2 %copy-start.8 = (f32[256]{0:T(256)S(1)}, f32[256]{0:T(256)}, u32[]{:S(2)}) copy-start(f32[256]{0:T(256)} %weight_ref.2) | copy-start | bytes 3076
  9.8 10.7 %copy-start.4 = (s32[64]{0:T(128)S(1)}, s32[64]{0:T(128)}, u32[]{:S(2)}) copy-start(s32[64]{0:T(128)} %cells_ref.2) | copy-start | bytes 772
  9.8 10.7 %copy-start.5 = (f32[64]{0:T(128)S(1)}, f32[64]{0:T(128)}, u32[]{:S(2)}) copy-start(f32[64]{0:T(128)} %rate_ref.1) | copy-start | bytes 772
  9.9 12.4 %copy-start.3 = (f32[8,128,128]{2,1,0:T(8,128)S(1)}, f32[8,128,128]{2,1,0:T(8,128)}, u32[]{:S(2)}) copy-start(f32[8,128,128]{2,1,0:T(8,128)} %weight_ref.3) | copy-start | bytes 1572868
  9.9 12.4 %copy-start.2 = (f32[8,128,128]{2,1,0:T(8,128)S(1)}, f32[8,128,128]{2,1,0:T(8,128)}, u32[]{:S(2)}) copy-start(f32[8,128,128]{2,1,0:T(8,128)} %survey_ref.1) | copy-start | bytes 1572868
  9.9 12.3 %collective-permute-start.2 = (f32[2,12,2,128]{3,2,1,0:T(2,128)S(1)}, f32[2,12,2,128]{3,2,1,0:T(2,128)S(1)}, u32[]{:S(2)}, u32[]{:S(2)}) collective-permute-start(f32[2,12,2,128]{3,2,1,0:T(2,128)S(1)} %get-tuple-element.36), channel_id=1, source_target_pairs={{1,2},{2,1},{5,6},{6,5},{9,10},{10,9},{13,14},{14,13},{17,18},{18,... | collective-permute-start | bytes 73736 | tf_op jit(solution)/shard_map/ppermute | solution.py:617
  10.7 11.5 %collective-permute-start.3 = (f32[2,12,2,128]{3,2,1,0:T(2,128)S(1)}, f32[2,12,2,128]{3,2,1,0:T(2,128)S(1)}, u32[]{:S(2)}, u32[]{:S(2)}) collective-permute-start(f32[2,12,2,128]{3,2,1,0:T(2,128)S(1)} %get-tuple-element.37), channel_id=1, source_target_pairs={{0,1},{2,3},{1,0},{3,2},{4,5},{6,7},{5,4},{7,6},{8,9},{10,11},{9,8... | collective-permute-start | bytes 73736 | tf_op jit(solution)/shard_map/ppermute | solution.py:618
  27.0 60.4 %collective-permute-start.4 = (f32[2,128,128]{2,1,0:T(8,128)}, f32[2,128,128]{2,1,0:T(8,128)S(1)}, u32[]{:S(2)}, u32[]{:S(2)}) collective-permute-start(f32[2,128,128]{2,1,0:T(8,128)} %get-tuple-element.42), channel_id=1, source_target_pairs={{4,8},{12,16},{20,24},{28,32},{36,40},{44,48},{52,56},{60,64},{68,... | collective-permute-start | bytes 393224 | tf_op jit(solution)/shard_map/ppermute | solution.py:617
  27.7 59.7 %collective-permute-start.5 = (f32[2,128,128]{2,1,0:T(8,128)}, f32[2,128,128]{2,1,0:T(8,128)S(1)}, u32[]{:S(2)}, u32[]{:S(2)}) collective-permute-start(f32[2,128,128]{2,1,0:T(8,128)} %get-tuple-element.43), channel_id=1, source_target_pairs={{0,4},{8,12},{16,20},{24,28},{32,36},{40,44},{48,52},{56,60},{64,6... | collective-permute-start | bytes 393224 | tf_op jit(solution)/shard_map/ppermute | solution.py:618
  41.5 67.5 %all-to-all-start.1 = ((f32[32,1,128]{2,1,0:T(1,128)}), f32[32,1,128]{2,1,0:T(1,128)S(1)}, u32[]{:S(2)}, u32[]{:S(2)}) async-start(f32[32,1,128]{2,1,0:T(1,128)} %shard_map.136), calls=%async_computation.1 | async-start | bytes 32768 | tf_op jit(solution)/shard_map/all_to_all | solution.py:710
  87.4 22.2 %collective-permute-start.6 = (f32[12,2,128]{2,1,0:T(2,128)S(1)}, f32[12,2,128]{2,1,0:T(2,128)S(1)}, u32[]{:S(2)}, u32[]{:S(2)}) collective-permute-start(f32[12,2,128]{2,1,0:T(2,128)S(1)} %get-tuple-element.44), channel_id=1, source_target_pairs={{1,2},{2,1},{5,6},{6,5},{9,10},{10,9},{13,14},{14,13},{17,18},{18,... | collective-permute-start | bytes 36872 | tf_op jit(solution)/shard_map/ppermute | solution.py:617
  88.1 21.5 %collective-permute-start.7 = (f32[12,2,128]{2,1,0:T(2,128)S(1)}, f32[12,2,128]{2,1,0:T(2,128)S(1)}, u32[]{:S(2)}, u32[]{:S(2)}) collective-permute-start(f32[12,2,128]{2,1,0:T(2,128)S(1)} %get-tuple-element.45), channel_id=1, source_target_pairs={{0,1},{2,3},{1,0},{3,2},{4,5},{6,7},{5,4},{7,6},{8,9},{10,11},{9,8... | collective-permute-start | bytes 36872 | tf_op jit(solution)/shard_map/ppermute | solution.py:618
